TPU v7x, 128 devices: a whole 4x4x4 slice. The times are simulated.
128 devices in a mesh: stage: 1, model: 16 (over z, y), data: 8 (over x, core).
Axes of the slice: x: 4, y: 4, z: 4, core: 2. Of those that a mesh axis runs over, the one named last changes fastest.
Arguments:
- w_fc1: float32 [16, 1024, 1024], P('stage', 'data', 'model')
- m_fc1: float32 [16, 1024, 1024], P('stage', 'data', 'model')
- g_fc1: bfloat16 [16, 1024, 1024], P('stage', 'data', 'model')
- w_fc2: float32 [16, 1024, 512], P('stage', 'data', 'model')
- m_fc2: float32 [16, 1024, 512], P('stage', 'data', 'model')
- g_fc2: bfloat16 [16, 1024, 512], P('stage', 'data', 'model')
Outputs:
- output 1: float32 [16, 1024, 1024], P('stage', 'data', 'model')
- output 2: float32 [16, 1024, 1024], P('stage', 'data', 'model')
- output 3: float32 [16, 1024, 512], P('stage', 'data', 'model')
- output 4: float32 [16, 1024, 512], P('stage', 'data', 'model')
All inputs are finite; a program needn't handle non-finite values.
Results may differ from a plain program's by a relative error of at most 0.00763347.
Values are sent between devices in bfloat16 or wider.
A program may use at most 1 GiB of HBM per device.

v0:
```python
import math
import jax
import jax.numpy as jnp
from jax import lax
from jax.sharding import PartitionSpec as P

NS_STEPS = 5
NS_COEF_A = 3.4445
NS_COEF_B = -4.7750
NS_COEF_C = 2.0315
MOMENTUM = 0.95
LEARN_RATE = 0.04
DECAY = 0.2
NORM_EPS = 1e-7


def newton_schulz(x_mat):
    row_count, col_count = x_mat.shape[1], x_mat.shape[2]
    for ns_step in range(NS_STEPS):
        if row_count <= col_count:
            gram_mat = jnp.einsum('emk,enk->emn', x_mat, x_mat, preferred_element_type=jnp.float32).astype(jnp.bfloat16)
        else:
            gram_mat = jnp.einsum('ekm,ekn->emn', x_mat, x_mat, preferred_element_type=jnp.float32).astype(jnp.bfloat16)
        gram_sq = jnp.einsum('emk,ekn->emn', gram_mat, gram_mat, preferred_element_type=jnp.float32)
        poly_mat = (NS_COEF_B * gram_mat.astype(jnp.float32) + NS_COEF_C * gram_sq).astype(jnp.bfloat16)
        if row_count <= col_count:
            update_term = jnp.einsum('emk,ekn->emn', poly_mat, x_mat, preferred_element_type=jnp.float32)
        else:
            update_term = jnp.einsum('emk,ekn->emn', x_mat, poly_mat, preferred_element_type=jnp.float32)
        x_mat = (NS_COEF_A * x_mat.astype(jnp.float32) + update_term).astype(jnp.bfloat16)
    return x_mat


def update_stack(w_loc, m_loc, g_loc, data_size, model_size):
    new_mom = MOMENTUM * m_loc + g_loc.astype(jnp.float32)
    mat_norms = jnp.sqrt(lax.psum(jnp.sum(new_mom * new_mom, axis=(1, 2)), ('data', 'model')))
    expert_count, rows_loc, cols_loc = m_loc.shape
    own_count = expert_count // data_size
    rows_full = rows_loc * data_size
    cols_full = cols_loc * model_size
    row_whole = lax.all_to_all(new_mom.astype(jnp.bfloat16), 'data', 0, 1, tiled=True)
    mom_whole = lax.all_gather(row_whole, 'model', axis=2, tiled=True)
    own_norms = lax.dynamic_slice_in_dim(mat_norms, lax.axis_index('data') * own_count, own_count)
    x_mat = (mom_whole.astype(jnp.float32) / (own_norms[:, None, None] + NORM_EPS)).astype(jnp.bfloat16)
    x_mat = newton_schulz(x_mat)
    x_cols = lax.dynamic_slice_in_dim(x_mat, lax.axis_index('model') * cols_loc, cols_loc, axis=2)
    x_back = lax.all_to_all(x_cols, 'data', 1, 0, tiled=True)
    step_scale = 0.2 * math.sqrt(max(rows_full, cols_full))
    new_w = w_loc - LEARN_RATE * (x_back.astype(jnp.float32) * step_scale + DECAY * w_loc)
    return new_w, new_mom


def solution(mesh):
    data_size = mesh.shape['data']
    model_size = mesh.shape['model']
    block_spec = P('stage', 'data', 'model')

    def local_step(w_fc1, m_fc1, g_fc1, w_fc2, m_fc2, g_fc2):
        new_w1, new_m1 = update_stack(w_fc1, m_fc1, g_fc1, data_size, model_size)
        new_w2, new_m2 = update_stack(w_fc2, m_fc2, g_fc2, data_size, model_size)
        return new_w1, new_m1, new_w2, new_m2

    return jax.shard_map(local_step, mesh=mesh, in_specs=(block_spec,) * 6, out_specs=(block_spec,) * 4, check_vma=False)
```

profile of v0, /device:TPU:96, one launch (start us, length us, event | category | flops | bytes accessed | tf_op | source)
XLA Modules:
  0.0 305.7 jit_solution(11420007427938291286)
XLA Ops:
  7.2 1.1 fusion.56
  8.3 10.2 %all_to_all.54 = bf16[16,128,32]{1,2,0:T(8,128)(2,1)S(1)} all-to-all(bf16[16,128,32]{1,2,0:T(8,128)(2,1)S(1)} %get-tuple-element.6), channel_id=1, replica_groups=mesh['stage'=1,'model'=16,'data'=8] {'data'}, dimensions={0} | all-to-all | bytes 262144 | tf_op jit(solution)/shard_map/all_to_all | solution.py:41
  18.6 0.7 all_to_all.48
  19.4 1.3 multiply_reduce_fusion
  20.7 0.8 copy-done
  21.6 10.0 %all_to_all.55 = bf16[16,128,64]{1,2,0:T(8,128)(2,1)S(1)} all-to-all(bf16[16,128,64]{1,2,0:T(8,128)(2,1)S(1)} %convert_element_type.187), channel_id=1, replica_groups=mesh['stage'=1,'model'=16,'data'=8] {'data'}, dimensions={0} | all-to-all | bytes 524288 | tf_op jit(solution)/shard_map/all_to_all | solution.py:41
  31.6 0.2 copy.97
  31.8 0.8 all_to_all.43
  32.6 0.2 multiply_reduce_fusion.1
  32.8 64.8 %all-reduce = (f32[16]{0:T(128)S(1)}, f32[16]{0:T(128)S(1)}) all-reduce(f32[16]{0:T(128)S(1)} %get-tuple-element.8, f32[16]{0:T(128)S(1)} %multiply_reduce_fusion.1), channel_id=1, replica_groups=mesh['stage'=1,'model'=16,'data'=8] {'data','model'}, use_global_device_ids=true, to_apply=%region_1.0 | all-reduce | flops 32 | bytes 256 | tf_op jit(solution)/shard_map/psum | solution.py:36
  97.7 3.7 %convolution_convert_fusion.8 = bf16[2,512,512]{2,1,0:T(8,128)(2,1)S(1)} fusion(bf16[2,1024,512]{1,2,0:T(8,128)(2,1)} %all-gather.5.cloned.1.call-done, f32[2]{0:T(128)S(1)} %dynamic-slice_add_fusion.2), kind=kOutput, calls=%fused_computation.49 | convolution fusion | flops 1077411840 | bytes 3145736 | tf_op jit(solution)/shard_map/ekm,ekn->emn/dot_general | solution.py:23
  101.5 3.4 %add_convert_fusion.17 = bf16[2,1024,512]{1,2,0:T(8,128)(2,1)} fusion(bf16[2,512,512]{2,1,0:T(8,128)(2,1)S(1)} %convolution_convert_fusion.8, f32[2]{0:T(128)S(1)} %dynamic-slice_add_fusion.2, bf16[2,1024,512]{1,2,0:T(8,128)(2,1)S(1)} %copy-done.4), kind=kOutput, calls=%fused_computation.18 | convolution fusion | flops 1623719936 | bytes 5242888 | tf_op jit(solution)/shard_map/emk,ekn->emn/dot_general | solution.py:29
  104.9 3.7 %convolution_convert_fusion.7 = bf16[2,512,512]{2,1,0:T(8,128)(2,1)S(1)} fusion(bf16[2,1024,512]{1,2,0:T(8,128)(2,1)} %add_convert_fusion.17), kind=kOutput, calls=%fused_computation.48 | convolution fusion | flops 1074266112 | bytes 3145728 | tf_op jit(solution)/shard_map/ekm,ekn->emn/dot_general | solution.py:23
  108.6 3.2 %add_convert_fusion.16 = bf16[2,1024,512]{1,2,0:T(8,128)(2,1)} fusion(bf16[2,1024,512]{1,2,0:T(8,128)(2,1)S(1)} %copy-done.5, bf16[2,512,512]{2,1,0:T(8,128)(2,1)S(1)} %convolution_convert_fusion.7), kind=kOutput, calls=%fused_computation.17 | convolution fusion | flops 1617428480 | bytes 5242880 | tf_op jit(solution)/shard_map/emk,ekn->emn/dot_general | solution.py:29
  111.9 3.7 %convolution_convert_fusion.6 = bf16[2,512,512]{2,1,0:T(8,128)(2,1)S(1)} fusion(bf16[2,1024,512]{1,2,0:T(8,128)(2,1)} %add_convert_fusion.16), kind=kOutput, calls=%fused_computation.47 | convolution fusion | flops 1074266112 | bytes 3145728 | tf_op jit(solution)/shard_map/ekm,ekn->emn/dot_general | solution.py:23
  115.5 3.2 %add_convert_fusion.15 = bf16[2,1024,512]{1,2,0:T(8,128)(2,1)} fusion(bf16[2,1024,512]{1,2,0:T(8,128)(2,1)S(1)} %copy-done.6, bf16[2,512,512]{2,1,0:T(8,128)(2,1)S(1)} %convolution_convert_fusion.6), kind=kOutput, calls=%fused_computation.16 | convolution fusion | flops 1617428480 | bytes 5242880 | tf_op jit(solution)/shard_map/emk,ekn->emn/dot_general | solution.py:29
  118.8 3.5 %convolution_convert_fusion.5 = bf16[2,512,512]{2,1,0:T(8,128)(2,1)S(1)} fusion(bf16[2,1024,512]{1,2,0:T(8,128)(2,1)} %add_convert_fusion.15), kind=kOutput, calls=%fused_computation.46 | convolution fusion | flops 1074266112 | bytes 3145728 | tf_op jit(solution)/shard_map/ekm,ekn->emn/dot_general | solution.py:23
  122.3 4.1 %add_convert_fusion.14 = bf16[2,1024,512]{1,2,0:T(8,128)(2,1)S(1)} fusion(bf16[2,1024,512]{1,2,0:T(8,128)(2,1)} %add_convert_fusion.15, bf16[2,512,512]{2,1,0:T(8,128)(2,1)S(1)} %convolution_convert_fusion.5), kind=kOutput, calls=%fused_computation.15 | convolution fusion | flops 1617428480 | bytes 5242880 | tf_op jit(solution)/shard_map/emk,ekn->emn/dot_general | solution.py:29
  126.4 1.5 convolution_convert_fusion.4
  127.9 3.9 %fusion.27 = f32[2,1024,512]{1,2,0:T(8,128)} fusion(bf16[2,1024,512]{1,2,0:T(8,128)(2,1)S(1)} %add_convert_fusion.14, bf16[2,512,512]{2,1,0:T(8,128)(2,1)S(1)} %convolution_convert_fusion.4), kind=kOutput, calls=%fused_computation.50 | convolution fusion | flops 1613234176 | bytes 7340032 | tf_op jit(solution)/shard_map/emk,ekn->emn/dot_general | solution.py:29
  131.8 1.0 fusion.33
  132.8 0.4 copy.68
  133.2 1.2 reshape.26
  134.4 3.4 %all-to-all-start.3 = ((bf16[8,2,4096]{2,1,0:T(2,128)(2,1)}), bf16[8,2,4096]{2,1,0:T(2,128)(2,1)S(1)}, u32[]{:S(2)}, u32[]{:S(2)}) async-start(bf16[8,2,4096]{2,1,0:T(2,128)(2,1)} %reshape.26), calls=%async_computation.3 | async-start | bytes 262144 | tf_op jit(solution)/shard_map/all_to_all | solution.py:47
  137.8 5.7 %all-to-all-done.3 = bf16[8,2,4096]{2,1,0:T(2,128)(2,1)S(1)} async-done(((bf16[8,2,4096]{2,1,0:T(2,128)(2,1)}), bf16[8,2,4096]{2,1,0:T(2,128)(2,1)S(1)}, u32[]{:S(2)}, u32[]{:S(2)}) %all-to-all-start.3) | async-done | bytes 131104 | tf_op jit(solution)/shard_map/all_to_all | solution.py:47
  143.6 0.3 reshape.27
  143.8 0.5 convert_multiply_fusion
  144.4 0.4 copy.69
  144.8 10.4 %convolution_convert_fusion.3 = bf16[2,1024,1024]{2,1,0:T(8,128)(2,1)} fusion(bf16[2,1024,1024]{1,2,0:T(8,128)(2,1)} %all-gather.3.cloned.1.call-done, f32[2]{0:T(128)S(1)} %dynamic-slice_add_fusion.3), kind=kOutput, calls=%fused_computation.35 | convolution fusion | flops 4303355904 | bytes 8388616 | tf_op jit(solution)/shard_map/emk,enk->emn/dot_general | solution.py:21
  155.2 17.9 %add_convert_fusion.7 = bf16[2,1024,1024]{1,2,0:T(8,128)(2,1)} fusion(bf16[2,1024,1024]{2,1,0:T(8,128)(2,1)} %convolution_convert_fusion.3, f32[2]{0:T(128)S(1)} %dynamic-slice_add_fusion.3, bf16[2,1024,1024]{1,2,0:T(8,128)(2,1)} %all-gather.3.cloned.1.call-done), kind=kOutput, calls=%fused_computation.7 | convolution fusion | flops 8621391872 | bytes 12582920 | tf_op jit(solution)/shard_map/emk,ekn->emn/dot_general | solution.py:27
  173.2 10.0 %convolution_convert_fusion.2 = bf16[2,1024,1024]{2,1,0:T(8,128)(2,1)} fusion(bf16[2,1024,1024]{1,2,0:T(8,128)(2,1)} %add_convert_fusion.7), kind=kOutput, calls=%fused_computation.34 | convolution fusion | flops 4297064448 | bytes 8388608 | tf_op jit(solution)/shard_map/emk,enk->emn/dot_general | solution.py:21
  183.2 18.2 %add_convert_fusion.5 = bf16[2,1024,1024]{1,2,0:T(8,128)(2,1)} fusion(bf16[2,1024,1024]{1,2,0:T(8,128)(2,1)} %add_convert_fusion.7, bf16[2,1024,1024]{2,1,0:T(8,128)(2,1)} %convolution_convert_fusion.2), kind=kOutput, calls=%fused_computation.5 | convolution fusion | flops 8608808960 | bytes 12582912 | tf_op jit(solution)/shard_map/emk,ekn->emn/dot_general | solution.py:27
  201.4 10.0 %convolution_convert_fusion.1 = bf16[2,1024,1024]{2,1,0:T(8,128)(2,1)} fusion(bf16[2,1024,1024]{1,2,0:T(8,128)(2,1)} %add_convert_fusion.5), kind=kOutput, calls=%fused_computation.33 | convolution fusion | flops 4297064448 | bytes 8388608 | tf_op jit(solution)/shard_map/emk,enk->emn/dot_general | solution.py:21
  211.4 17.8 %add_convert_fusion.3 = bf16[2,1024,1024]{1,2,0:T(8,128)(2,1)} fusion(bf16[2,1024,1024]{1,2,0:T(8,128)(2,1)} %add_convert_fusion.5, bf16[2,1024,1024]{2,1,0:T(8,128)(2,1)} %convolution_convert_fusion.1), kind=kOutput, calls=%fused_computation.3 | convolution fusion | flops 8608808960 | bytes 12582912 | tf_op jit(solution)/shard_map/emk,ekn->emn/dot_general | solution.py:27
  229.2 10.0 %convolution_convert_fusion = bf16[2,1024,1024]{2,1,0:T(8,128)(2,1)} fusion(bf16[2,1024,1024]{1,2,0:T(8,128)(2,1)} %add_convert_fusion.3), kind=kOutput, calls=%fused_computation.32 | convolution fusion | flops 4297064448 | bytes 8388608 | tf_op jit(solution)/shard_map/emk,enk->emn/dot_general | solution.py:21
  239.2 17.5 %add_convert_fusion.1 = bf16[2,1024,1024]{1,2,0:T(8,128)(2,1)} fusion(bf16[2,1024,1024]{1,2,0:T(8,128)(2,1)} %add_convert_fusion.3, bf16[2,1024,1024]{2,1,0:T(8,128)(2,1)} %convolution_convert_fusion), kind=kOutput, calls=%fused_computation.1 | convolution fusion | flops 8608808960 | bytes 12582912 | tf_op jit(solution)/shard_map/emk,ekn->emn/dot_general | solution.py:27
  256.6 10.0 %fusion.57 = bf16[2,1024,1024]{2,1,0:T(8,128)(2,1)} fusion(bf16[2,1024,1024]{1,2,0:T(8,128)(2,1)} %add_convert_fusion.1), kind=kOutput, calls=%fused_computation.94 | convolution fusion | flops 4294967296 | bytes 8388608 | tf_op jit(solution)/shard_map/emk,enk->emn/dot_general | solution.py:21
  266.6 16.2 %fusion.4 = f32[2,1024,1024]{1,2,0:T(8,128)} fusion(bf16[2,1024,1024]{1,2,0:T(8,128)(2,1)} %add_convert_fusion.1, bf16[2,1024,1024]{2,1,0:T(8,128)(2,1)} %fusion.57), kind=kOutput, calls=%fused_computation.14 | convolution fusion | flops 8600420352 | bytes 16777216 | tf_op jit(solution)/shard_map/emk,ekn->emn/dot_general | solution.py:27
  282.8 1.2 fusion.30
  284.1 0.4 copy.50
  284.5 1.1 reshape.24
  285.6 3.4 %all-to-all-start.1 = ((bf16[8,2,8192]{2,1,0:T(2,128)(2,1)}), bf16[8,2,8192]{2,1,0:T(2,128)(2,1)S(1)}, u32[]{:S(2)}, u32[]{:S(2)}) async-start(bf16[8,2,8192]{2,1,0:T(2,128)(2,1)} %reshape.24), calls=%async_computation.1 | async-start | bytes 524288 | tf_op jit(solution)/shard_map/all_to_all | solution.py:47
  289.0 0.8 fusion.35
  289.8 6.6 %all-to-all-done.1 = bf16[8,2,8192]{2,1,0:T(2,128)(2,1)S(1)} async-done(((bf16[8,2,8192]{2,1,0:T(2,128)(2,1)}), bf16[8,2,8192]{2,1,0:T(2,128)(2,1)S(1)}, u32[]{:S(2)}, u32[]{:S(2)}) %all-to-all-start.1) | async-done | bytes 262176 | tf_op jit(solution)/shard_map/all_to_all | solution.py:47
  296.4 0.3 reshape.25
  296.7 0.5 convert_multiply_fusion.1
  297.3 0.5 copy.51
  297.7 0.9 fusion.32
  (25 shorter events, 0.5 us)
Async XLA Ops:
  7.2 90.6 %all-gather.5.cloned.1.call-start = ((), (), s32[]{:S(2)}) async-start(), calls=%async_computation.5 | async-start | bytes 2228224 | tf_op jit(solution)/shard_map/all_gather | solution.py:42
  8.3 93.2 %copy-start.1 = (f32[16,128,32]{1,2,0:T(8,128)}, f32[16,128,32]{1,2,0:T(8,128)S(1)}, u32[]{:S(2)}) copy-start(f32[16,128,32]{1,2,0:T(8,128)S(1)} %get-tuple-element.7) | copy-start | bytes 786436
  19.3 125.5 %all-gather.3.cloned.1.call-start = ((), (), s32[]{:S(2)}) async-start(), calls=%async_computation.4 | async-start | bytes 4456448 | tf_op jit(solution)/shard_map/all_gather | solution.py:42
  20.7 0.8 copy-start
  97.7 3.8 %copy-start.4 = (bf16[2,1024,512]{1,2,0:T(8,128)(2,1)S(1)}, bf16[2,1024,512]{1,2,0:T(8,128)(2,1)}, u32[]{:S(2)}) copy-start(bf16[2,1024,512]{1,2,0:T(8,128)(2,1)} %all-gather.5.cloned.1.call-done) | copy-start | bytes 6291460
  104.9 3.7 %copy-start.5 = (bf16[2,1024,512]{1,2,0:T(8,128)(2,1)S(1)}, bf16[2,1024,512]{1,2,0:T(8,128)(2,1)}, u32[]{:S(2)}) copy-start(bf16[2,1024,512]{1,2,0:T(8,128)(2,1)} %add_convert_fusion.17) | copy-start | bytes 6291460
  111.9 3.7 %copy-start.6 = (bf16[2,1024,512]{1,2,0:T(8,128)(2,1)S(1)}, bf16[2,1024,512]{1,2,0:T(8,128)(2,1)}, u32[]{:S(2)}) copy-start(bf16[2,1024,512]{1,2,0:T(8,128)(2,1)} %add_convert_fusion.16) | copy-start | bytes 6291460
  134.4 9.2 %all-to-all-start.3 = ((bf16[8,2,4096]{2,1,0:T(2,128)(2,1)}), bf16[8,2,4096]{2,1,0:T(2,128)(2,1)S(1)}, u32[]{:S(2)}, u32[]{:S(2)}) async-start(bf16[8,2,4096]{2,1,0:T(2,128)(2,1)} %reshape.26), calls=%async_computation.3 | async-start | bytes 262144 | tf_op jit(solution)/shard_map/all_to_all | solution.py:47
  266.6 22.4 %copy-start.3 = (f32[16,128,32]{1,2,0:T(8,128)S(1)}, f32[16,128,32]{1,2,0:T(8,128)}, u32[]{:S(2)}) copy-start(f32[16,128,32]{1,2,0:T(8,128)} %param.9) | copy-start | bytes 786436
  282.8 14.9 %copy-start.2 = (f32[16,128,64]{1,2,0:T(8,128)S(1)}, f32[16,128,64]{1,2,0:T(8,128)}, u32[]{:S(2)}) copy-start(f32[16,128,64]{1,2,0:T(8,128)} %param.6) | copy-start | bytes 1572868
  285.6 10.8 %all-to-all-start.1 = ((bf16[8,2,8192]{2,1,0:T(2,128)(2,1)}), bf16[8,2,8192]{2,1,0:T(2,128)(2,1)S(1)}, u32[]{:S(2)}, u32[]{:S(2)}) async-start(bf16[8,2,8192]{2,1,0:T(2,128)(2,1)} %reshape.24), calls=%async_computation.1 | async-start | bytes 524288 | tf_op jit(solution)/shard_map/all_to_all | solution.py:47
Sparse Core Ops, SparseCore 0:
  19.5 44.0 all-gather.4
  66.3 50.7 all-gather.2
where the time goes:
time: 311 us; the launch traced here: 306 us
  matrix products  172 us (55%)
  blocking collectives  85 us (27%)
  between operations  14.6 us (5%)
  waiting for transfers between devices  12.4 us (4%)
  other arithmetic  7.75 us (2%)
  local copies, waits for them, and re-layouts  7.15 us (2%)
  starting transfers between devices  6.87 us (2%)
    dot_general x5, matrix products, newton_schulz(): jnp.einsum('emk,ekn->emn', poly_mat, x_mat, preferred_element_type=jnp.fl...  87.6 us
    psum x1, blocking collectives, update_stack(): lax.psum(jnp.sum(new_mom * new_mom, axis=(1, 2)), ('data', 'model'))  64.8 us
    dot_general x5, matrix products, newton_schulz(): jnp.einsum('emk,enk->emn', x_mat, x_mat, preferred_element_type=jnp.float32)  50.4 us
    all_to_all x2, blocking collectives, update_stack(): lax.all_to_all(new_mom.astype(jnp.bfloat16), 'data', 0, 1, tiled=True)  20.2 us
    dot_general x5, matrix products, newton_schulz(): jnp.einsum('emk,ekn->emn', x_mat, poly_mat, preferred_element_type=jnp.fl...  17.9 us
    dot_general x5, matrix products, newton_schulz(): jnp.einsum('ekm,ekn->emn', x_mat, x_mat, preferred_element_type=jnp.float32)  16.1 us
    all_to_all x2, waiting for transfers between devices, update_stack(): x_back = lax.all_to_all(x_cols, 'data', 1, 0, tiled=True)  12.3 us
    all_to_all x2, starting transfers between devices, update_stack(): x_back = lax.all_to_all(x_cols, 'data', 1, 0, tiled=True)  6.78 us
  transfers between devices with their start and end apart: 4, of which 2 were waited for; matrix products, arithmetic and copies ran while one was open for 13% of the time, Pallas kernels for 0%

commit v1 on v0

v1 whole, which is shorter than its diff:
```python
import functools
import math
import jax
import jax.numpy as jnp
from jax import lax
from jax.experimental import pallas as pl
from jax.experimental.pallas import tpu as pltpu
from jax.sharding import PartitionSpec as P

NS_STEPS = 5
NS_COEF_A = 3.4445
NS_COEF_B = -4.7750
NS_COEF_C = 2.0315
MOMENTUM = 0.95
LEARN_RATE = 0.04
DECAY = 0.2
NORM_EPS = 1e-7

BF16 = jnp.bfloat16
F32 = jnp.float32
NN = ((1,), (0,))
TN = ((0,), (0,))
NT = ((1,), (1,))
MESH = pl.DeviceIdType.MESH


def dot(lhs, rhs, dims):
    return lax.dot_general(lhs, rhs, (dims, ((), ())), preferred_element_type=F32)


def muon_kernel(m1_hbm, g1_hbm, m2_hbm, g2_hbm, res1, res2,
                m1, g1, m2, g2, send1, send2, part1, part2,
                raw1, raw2, norms, y_own, y_oth, a_own, a_cross, a_oth, b_own, b_cross, y2, a2, b2,
                in_sem, send_sem, gather_sem, norm_sem, result_sem, y_send, y_recv, a_send, a_recv, out_send):
    midx = lax.axis_index('model')
    didx = lax.axis_index('data')
    core = didx % 2
    xpos = didx // 2
    diag = midx // 4 + midx % 4
    flat = midx * 8 + didx
    is_own1 = (8 - diag) % 4 == xpos
    is_own2 = jnp.logical_and((10 - diag) % 4 == xpos, core == 1)

    def to(model, data):
        return {'model': model, 'data': data}

    loads = [pltpu.make_async_copy(src, dst, in_sem.at[i])
             for i, (src, dst) in enumerate(((m1_hbm, m1), (g1_hbm, g1), (m2_hbm, m2), (g2_hbm, g2)))]
    for load in loads:
        load.start()

    barrier = pltpu.get_barrier_semaphore()

    def greet(i, carry):
        other = (flat + i) % 128
        pl.semaphore_signal(barrier, inc=1, device_id=to(other // 8, other % 8), device_id_type=MESH)
        return carry

    lax.fori_loop(1, 128, greet, 0)

    def momentum(e, carry, m_ref, g_ref, send, part):
        value = MOMENTUM * m_ref[e] + g_ref[e].astype(F32)
        send[e] = value.astype(BF16)
        part[e] = jnp.sum(value * value, axis=0, keepdims=True)
        return carry

    loads[0].wait()
    loads[1].wait()
    lax.fori_loop(0, 16, functools.partial(momentum, m_ref=m1, g_ref=g1, send=send1, part=part1), 0)
    loads[2].wait()
    loads[3].wait()
    lax.fori_loop(0, 16, functools.partial(momentum, m_ref=m2, g_ref=g2, send=send2, part=part2), 0)
    pl.semaphore_wait(barrier, 127)

    def send_fc1(i, carry):
        e = (midx + 2 * didx + i) % 16
        ox = (8 - e // 4 - e % 4) % 4
        mine = jnp.logical_and(e == midx, is_own1)
        for side in range(2):
            @pl.when(jnp.logical_not(jnp.logical_and(mine, core == side)))
            def _():
                pltpu.make_async_remote_copy(
                    part1.at[e], norms.at[flat], send_sem.at[1], norm_sem,
                    device_id=to(e, 2 * ox + side), device_id_type=MESH).start()

        @pl.when(jnp.logical_not(mine))
        def _():
            pltpu.make_async_remote_copy(
                send1.at[e], raw1.at[xpos * 16 + midx], send_sem.at[0], gather_sem.at[xpos // 2],
                device_id=to(e, 2 * ox + core), device_id_type=MESH).start()
        return carry

    lax.fori_loop(0, 16, send_fc1, 0)

    def send_fc2(i, carry):
        e = (midx + 2 * didx + i) % 16
        ox = (10 - e // 4 - e % 4) % 4

        @pl.when(jnp.logical_not(jnp.logical_and(e == midx, is_own2)))
        def _():
            pltpu.make_async_remote_copy(
                part2.at[e], norms.at[flat], send_sem.at[3], norm_sem,
                device_id=to(e, 2 * ox + 1), device_id_type=MESH).start()
            pltpu.make_async_remote_copy(
                send2.at[e], raw2.at[flat], send_sem.at[2], gather_sem.at[0],
                device_id=to(e, 2 * ox + 1), device_id_type=MESH).start()
        return carry

    lax.fori_loop(0, 16, send_fc2, 0)

    def wait_for(ref, sem):
        pltpu.make_async_copy(ref, ref, sem).wait()

    def denominator():
        wait_for(norms.at[pl.ds(0, 127)], norm_sem)
        total = jnp.sum(jnp.sum(norms[...], axis=0), axis=1, keepdims=True)
        return jnp.sqrt(total) + NORM_EPS

    @pl.when(is_own1)
    def _():
        partner = to(midx, 2 * xpos + 1 - core)
        norms[flat] = part1[midx]
        raw1[xpos * 16 + midx] = send1[midx]
        den = denominator()

        def push(slot, half):
            return pltpu.make_async_remote_copy(
                y_own.at[slot, :, pl.ds(half * 256, 256)], y_oth.at[slot, :, pl.ds(half * 256, 256)],
                y_send.at[slot, half], y_recv.at[slot, half], device_id=partner, device_id_type=MESH)

        def push_gram(slot):
            return pltpu.make_async_remote_copy(
                a_own.at[slot], a_oth.at[slot], a_send.at[slot], a_recv.at[slot],
                device_id=partner, device_id_type=MESH)

        for half in range(2):
            @pl.when(xpos // 2 == half)
            def _():
                wait_for(raw1.at[pl.ds(0, 31)], gather_sem.at[half])

            @pl.when(xpos // 2 != half)
            def _():
                wait_for(raw1.at[pl.ds(0, 32)], gather_sem.at[half])

            def scale(k, carry):
                for lane in (2 * half, 2 * half + 1):
                    block = raw1[lane * 16 + k].astype(F32) / den
                    y_own[0, pl.ds(k * 64, 64), lane * 128:(lane + 1) * 128] = block.astype(BF16)
                return carry

            lax.fori_loop(0, 16, scale, 0)
            push(0, half).start()

        def step(k, carry):
            now = k % 2
            nxt = 1 - now
            a_own[now] = dot(y_own[now], y_own[now], TN).astype(BF16)
            push_gram(now).start()
            for half in range(2):
                push(now, half).wait()
            a_cross[...] = dot(y_oth[now], y_own[now], TN).astype(BF16)
            own_sq = dot(a_own[now], a_own[now], NN) + dot(a_cross[...], a_cross[...], TN)
            b_own[...] = (NS_COEF_B * a_own[now].astype(F32) + NS_COEF_C * own_sq).astype(BF16)
            push_gram(now).wait()
            cross_sq = dot(a_cross[...], a_own[now], NN) + dot(a_oth[now], a_cross[...], NN)
            b_cross[...] = (NS_COEF_B * a_cross[...].astype(F32) + NS_COEF_C * cross_sq).astype(BF16)
            for half in range(2):
                lanes = slice(half * 256, (half + 1) * 256)
                update = dot(y_own[now], b_own[:, lanes], NN) + dot(y_oth[now], b_cross[:, lanes], NN)
                y_own[nxt, :, lanes] = (NS_COEF_A * y_own[now, :, lanes].astype(F32) + update).astype(BF16)

                @pl.when(k < NS_STEPS - 1)
                def _():
                    push(nxt, half).start()

                @pl.when(k == NS_STEPS - 1)
                def _():
                    def scatter(i, carry):
                        mm = (midx + i) % 16
                        for lane in (2 * half, 2 * half + 1):
                            @pl.when(jnp.logical_not(jnp.logical_and(mm == midx, lane == xpos)))
                            def _():
                                pltpu.make_async_remote_copy(
                                    y_own.at[nxt, pl.ds(mm * 64, 64), pl.ds(lane * 128, 128)], res1.at[midx],
                                    out_send, result_sem.at[0],
                                    device_id=to(mm, 2 * lane + core), device_id_type=MESH).start()
                        return carry
                    lax.fori_loop(0, 16, scatter, 0)
            return carry

        lax.fori_loop(0, NS_STEPS, step, 0)
        for lane in range(4):
            @pl.when(xpos == lane)
            def _():
                res1[midx] = y_own[NS_STEPS % 2, pl.ds(midx * 64, 64), lane * 128:(lane + 1) * 128]
        wait_for(raw1.at[pl.ds(0, 63)], out_send)
        wait_for(send1.at[pl.ds(0, 15)], send_sem.at[0])
        wait_for(norms.at[pl.ds(0, 31)], send_sem.at[1])
        wait_for(res1.at[pl.ds(0, 15)], result_sem.at[0])

    @pl.when(jnp.logical_not(is_own1))
    def _():
        wait_for(send1, send_sem.at[0])
        wait_for(norms.at[pl.ds(0, 32)], send_sem.at[1])

    @pl.when(is_own2)
    def _():
        norms[flat] = part2[midx]
        raw2[flat] = send2[midx]
        den = denominator()
        wait_for(raw2.at[pl.ds(0, 127)], gather_sem.at[0])

        def scale(k, carry):
            for d in range(8):
                block = raw2[k * 8 + d].astype(F32) / den
                y2[pl.ds(k * 32, 32), d * 128:(d + 1) * 128] = block.astype(BF16)
            return carry

        lax.fori_loop(0, 16, scale, 0)

        def step(k, carry):
            a2[...] = dot(y2[...], y2[...], NT).astype(BF16)
            b2[...] = (NS_COEF_B * a2[...].astype(F32) + NS_COEF_C * dot(a2[...], a2[...], NN)).astype(BF16)
            y2[...] = (NS_COEF_A * y2[...].astype(F32) + dot(b2[...], y2[...], NN)).astype(BF16)
            return carry

        lax.fori_loop(0, NS_STEPS, step, 0)

        def scatter(i, carry):
            mm = (midx + i) % 16
            for d in range(8):
                @pl.when(jnp.logical_not(jnp.logical_and(mm == midx, didx == d)))
                def _():
                    pltpu.make_async_remote_copy(
                        y2.at[pl.ds(mm * 32, 32), pl.ds(d * 128, 128)], res2.at[midx], out_send, result_sem.at[1],
                        device_id=to(mm, d), device_id_type=MESH).start()
            return carry

        lax.fori_loop(0, 16, scatter, 0)
        for d in range(8):
            @pl.when(didx == d)
            def _():
                res2[midx] = y2[pl.ds(midx * 32, 32), d * 128:(d + 1) * 128]
        wait_for(raw2.at[pl.ds(0, 127)], out_send)
        wait_for(send2.at[pl.ds(0, 15)], send_sem.at[2])
        wait_for(norms.at[pl.ds(0, 15)], send_sem.at[3])
        wait_for(res2.at[pl.ds(0, 15)], result_sem.at[1])

    @pl.when(jnp.logical_not(is_own2))
    def _():
        wait_for(send2, send_sem.at[2])
        wait_for(norms.at[pl.ds(0, 16)], send_sem.at[3])
        wait_for(res2, result_sem.at[1])

    @pl.when(jnp.logical_not(is_own1))
    def _():
        wait_for(res1, result_sem.at[0])


def exchange(m1, g1, m2, g2):
    hbm_spec = pl.BlockSpec(memory_space=pltpu.HBM)
    vmem_spec = pl.BlockSpec(memory_space=pltpu.VMEM)
    vmem = pltpu.VMEM
    sem = pltpu.SemaphoreType.DMA
    return pl.pallas_call(
        muon_kernel,
        out_shape=(jax.ShapeDtypeStruct((16, 64, 128), BF16), jax.ShapeDtypeStruct((16, 32, 128), BF16)),
        in_specs=[hbm_spec] * 4,
        out_specs=(vmem_spec, vmem_spec),
        scratch_shapes=[
            vmem((16, 64, 128), F32), vmem((16, 64, 128), BF16), vmem((16, 32, 128), F32), vmem((16, 32, 128), BF16),
            vmem((16, 64, 128), BF16), vmem((16, 32, 128), BF16), vmem((16, 1, 128), F32), vmem((16, 1, 128), F32),
            vmem((64, 64, 128), BF16), vmem((128, 32, 128), BF16), vmem((128, 1, 128), F32),
            vmem((2, 1024, 512), BF16), vmem((2, 1024, 512), BF16),
            vmem((2, 512, 512), BF16), vmem((512, 512), BF16), vmem((2, 512, 512), BF16),
            vmem((512, 512), BF16), vmem((512, 512), BF16),
            vmem((512, 1024), BF16), vmem((512, 512), BF16), vmem((512, 512), BF16),
            sem((4,)), sem((4,)), sem((2,)), sem, sem((2,)), sem((2, 2)), sem((2, 2)), sem((2,)), sem((2,)), sem,
        ],
        compiler_params=pltpu.CompilerParams(collective_id=0, has_side_effects=True, vmem_limit_bytes=48 << 20),
        name='muon_exchange',
    )(m1, g1, m2, g2)


def weight_step(weights, momentum, gradient, ortho_t, rows, cols):
    new_mom = MOMENTUM * momentum + gradient.astype(F32)
    ortho = jnp.swapaxes(ortho_t, 1, 2).astype(F32) * (0.2 * math.sqrt(max(rows, cols)))
    return weights - LEARN_RATE * (ortho + DECAY * weights), new_mom


def solution(mesh):
    block_spec = P('stage', 'data', 'model')

    def local_step(w1, m1, g1, w2, m2, g2):
        flip = functools.partial(jnp.swapaxes, axis1=1, axis2=2)
        ortho1, ortho2 = exchange(flip(m1), flip(g1), flip(m2), flip(g2))
        new_w1, new_m1 = weight_step(w1, m1, g1, ortho1, 1024, 1024)
        new_w2, new_m2 = weight_step(w2, m2, g2, ortho2, 1024, 512)
        return new_w1, new_m1, new_w2, new_m2

    return jax.shard_map(local_step, mesh=mesh, in_specs=(block_spec,) * 6, out_specs=(block_spec,) * 4, check_vma=False)
```

time: 311 us -> 73.6 us (0.24)
  the two profiles are of different devices: /device:TPU:96 before, /device:TPU:6 now
where the time goes in v1:
time: 73.6 us; the launch traced here: 73.4 us
  Pallas kernels  66.8 us (91%)
  local copies, waits for them, and re-layouts  3.85 us (5%)
  other arithmetic  2.06 us (3%)
    pallas_call x1, Pallas kernels, exchange(): pl.pallas_call(muon_kernel, out_shape=(jax.ShapeDtypeStruct((16, 64, 128)...  66.8 us
    unnamed x12, local copies, waits for them, and re-layouts  3.85 us
    sub x2, other arithmetic, weight_step(): return (weights - LEARN_RATE * (ortho + DECAY * weights), new_mom)  2.06 us

profile of v1, /device:TPU:6, one launch (start us, length us, event | category | flops | bytes accessed | tf_op | source)
XLA Modules:
  0.0 73.4 jit_solution(10607397238628867853)
XLA Ops:
  0.6 0.0 copy-start
  0.6 1.0 %copy-done = f32[16,128,64]{1,2,0:T(8,128)S(1)} copy-done((f32[16,128,64]{1,2,0:T(8,128)S(1)}, f32[16,128,64]{1,2,0:T(8,128)}, u32[]{:S(2)}) %copy-start) | copy-done | bytes 524312
  1.7 0.0 copy-start.1
  1.7 0.9 %copy-done.1 = bf16[16,128,64]{1,2,0:T(8,128)(2,1)S(1)} copy-done((bf16[16,128,64]{1,2,0:T(8,128)(2,1)S(1)}, bf16[16,128,64]{1,2,0:T(8,128)(2,1)}, u32[]{:S(2)}) %copy-start.1) | copy-done | bytes 262168
  2.6 0.0 copy-start.2
  2.6 0.9 %copy-done.2 = f32[16,128,32]{1,2,0:T(8,128)S(1)} copy-done((f32[16,128,32]{1,2,0:T(8,128)S(1)}, f32[16,128,32]{1,2,0:T(8,128)}, u32[]{:S(2)}) %copy-start.2) | copy-done | bytes 262168
  3.6 0.0 copy-start.3
  3.6 0.9 %copy-done.3 = bf16[16,128,32]{1,2,0:T(8,128)(2,1)S(1)} copy-done((bf16[16,128,32]{1,2,0:T(8,128)(2,1)S(1)}, bf16[16,128,32]{1,2,0:T(8,128)(2,1)}, u32[]{:S(2)}) %copy-start.3) | copy-done | bytes 131096
  4.5 0.0 copy-start.4
  4.5 66.8 %muon_exchange.1 = (bf16[16,64,128]{2,1,0:T(8,128)(2,1)S(1)}, bf16[16,32,128]{2,1,0:T(8,128)(2,1)S(1)}) custom-call(f32[16,64,128]{2,1,0:T(8,128)S(1)} %bitcast.16, bf16[16,64,128]{2,1,0:T(8,128)(2,1)S(1)} %bitcast.17, f32[16,32,128]{2,1,0:T(8,128)S(1)} %bitcast.18, bf16[16,32,128]{2,1,0:T(8,128)(2,1)S(1)} %bitcast.19), custom_call_target="tpu_custom_call" | custom-call | tf_op jit(solution)/shard_map/muon_exchange/pallas_call | solution.py:265
  71.3 0.0 copy-done.4
  71.3 0.0 copy-start.5
  71.3 1.2 %fusion.1 = (f32[16,128,64]{1,2,0:T(8,128)}, f32[16,128,64]{1,2,0:T(8,128)}) fusion(f32[16,128,64]{1,2,0:T(8,128)S(1)} %copy-done.4, bf16[16,64,128]{2,1,0:T(8,128)(2,1)S(1)} %get-tuple-element.6, bf16[16,128,64]{1,2,0:T(8,128)(2,1)S(1)} %copy-done.1, f32[16,128,64]{1,2,0:T(8,128)S(1)} %copy-done), kind=kLoop, calls=%fused_computation.2 | loop fusion | flops 1179648 | bytes 2621440 | tf_op jit(solution)/shard_map/sub | solution.py:288
  72.5 0.0 copy-done.5
  72.5 0.9 %fusion.3 = (f32[16,128,32]{1,2,0:T(8,128)}, f32[16,128,32]{1,2,0:T(8,128)}) fusion(f32[16,128,32]{1,2,0:T(8,128)S(1)} %copy-done.5, bf16[16,32,128]{2,1,0:T(8,128)(2,1)S(1)} %get-tuple-element.7, bf16[16,128,32]{1,2,0:T(8,128)(2,1)S(1)} %copy-done.3, f32[16,128,32]{1,2,0:T(8,128)S(1)} %copy-done.2), kind=kLoop, calls=%fused_computation.6 | loop fusion | flops 589824 | bytes 1310720 | tf_op jit(solution)/shard_map/sub | solution.py:288
Async XLA Ops:
  0.6 1.0 %copy-start = (f32[16,128,64]{1,2,0:T(8,128)S(1)}, f32[16,128,64]{1,2,0:T(8,128)}, u32[]{:S(2)}) copy-start(f32[16,128,64]{1,2,0:T(8,128)} %param.7) | copy-start | bytes 1572868
  1.7 0.9 %copy-start.1 = (bf16[16,128,64]{1,2,0:T(8,128)(2,1)S(1)}, bf16[16,128,64]{1,2,0:T(8,128)(2,1)}, u32[]{:S(2)}) copy-start(bf16[16,128,64]{1,2,0:T(8,128)(2,1)} %param.8) | copy-start | bytes 786436
  2.6 0.9 %copy-start.2 = (f32[16,128,32]{1,2,0:T(8,128)S(1)}, f32[16,128,32]{1,2,0:T(8,128)}, u32[]{:S(2)}) copy-start(f32[16,128,32]{1,2,0:T(8,128)} %param.10) | copy-start | bytes 786436
  3.6 0.9 %copy-start.3 = (bf16[16,128,32]{1,2,0:T(8,128)(2,1)S(1)}, bf16[16,128,32]{1,2,0:T(8,128)(2,1)}, u32[]{:S(2)}) copy-start(bf16[16,128,32]{1,2,0:T(8,128)(2,1)} %param.11) | copy-start | bytes 393220
  4.5 66.8 %copy-start.4 = (f32[16,128,64]{1,2,0:T(8,128)S(1)}, f32[16,128,64]{1,2,0:T(8,128)}, u32[]{:S(2)}) copy-start(f32[16,128,64]{1,2,0:T(8,128)} %param.6) | copy-start | bytes 1572868
  71.3 1.2 %copy-start.5 = (f32[16,128,32]{1,2,0:T(8,128)S(1)}, f32[16,128,32]{1,2,0:T(8,128)}, u32[]{:S(2)}) copy-start(f32[16,128,32]{1,2,0:T(8,128)} %param.9) | copy-start | bytes 786436

commit v2 on v1

--- a/solution.py
+++ b/solution.py
@@ -30,7 +30,7 @@
 
 def muon_kernel(m1_hbm, g1_hbm, m2_hbm, g2_hbm, res1, res2,
                 m1, g1, m2, g2, send1, send2, part1, part2,
-                raw1, raw2, norms, y_own, y_oth, a_own, a_cross, a_oth, b_own, b_cross, y2, a2, b2,
+                raw1, raw2, norms, y_own, y_oth, a_own, a_cross, a_oth, b_own, b_cross, square, y2, a2, b2,
                 in_sem, send_sem, gather_sem, norm_sem, result_sem, y_send, y_recv, a_send, a_recv, out_send):
     midx = lax.axis_index('model')
     didx = lax.axis_index('data')
@@ -56,7 +56,11 @@
         pl.semaphore_signal(barrier, inc=1, device_id=to(other // 8, other % 8), device_id_type=MESH)
         return carry
 
-    lax.fori_loop(1, 128, greet, 0)
+    is_owner = jnp.logical_or(is_own1, is_own2)
+
+    @pl.when(is_owner)
+    def _():
+        lax.fori_loop(1, 128, greet, 0)
 
     def momentum(e, carry, m_ref, g_ref, send, part):
         value = MOMENTUM * m_ref[e] + g_ref[e].astype(F32)
@@ -70,7 +74,14 @@
     loads[2].wait()
     loads[3].wait()
     lax.fori_loop(0, 16, functools.partial(momentum, m_ref=m2, g_ref=g2, send=send2, part=part2), 0)
-    pl.semaphore_wait(barrier, 127)
+
+    @pl.when(is_owner)
+    def _():
+        pl.semaphore_wait(barrier, 47)
+
+    @pl.when(jnp.logical_not(is_owner))
+    def _():
+        pl.semaphore_wait(barrier, 48)
 
     def send_fc1(i, carry):
         e = (midx + 2 * didx + i) % 16
@@ -86,7 +97,7 @@
         @pl.when(jnp.logical_not(mine))
         def _():
             pltpu.make_async_remote_copy(
-                send1.at[e], raw1.at[xpos * 16 + midx], send_sem.at[0], gather_sem.at[xpos // 2],
+                send1.at[e], raw1.at[midx * 4 + xpos], send_sem.at[0], gather_sem.at[midx // 4],
                 device_id=to(e, 2 * ox + core), device_id_type=MESH).start()
         return carry
 
@@ -120,75 +131,84 @@
     def _():
         partner = to(midx, 2 * xpos + 1 - core)
         norms[flat] = part1[midx]
-        raw1[xpos * 16 + midx] = send1[midx]
+        raw1[midx * 4 + xpos] = send1[midx]
         den = denominator()
 
-        def push(slot, half):
+        def push(slot, q):
+            rows = (slot, pl.ds(q * 256, 256))
             return pltpu.make_async_remote_copy(
-                y_own.at[slot, :, pl.ds(half * 256, 256)], y_oth.at[slot, :, pl.ds(half * 256, 256)],
-                y_send.at[slot, half], y_recv.at[slot, half], device_id=partner, device_id_type=MESH)
+                y_own.at[rows], y_oth.at[rows], y_send.at[slot, q], y_recv.at[slot, q],
+                device_id=partner, device_id_type=MESH)
 
         def push_gram(slot):
             return pltpu.make_async_remote_copy(
                 a_own.at[slot], a_oth.at[slot], a_send.at[slot], a_recv.at[slot],
                 device_id=partner, device_id_type=MESH)
 
-        for half in range(2):
-            @pl.when(xpos // 2 == half)
-            def _():
-                wait_for(raw1.at[pl.ds(0, 31)], gather_sem.at[half])
-
-            @pl.when(xpos // 2 != half)
-            def _():
-                wait_for(raw1.at[pl.ds(0, 32)], gather_sem.at[half])
+        for q in range(4):
+            @pl.when(midx // 4 == q)
+            def _():
+                wait_for(raw1.at[pl.ds(0, 15)], gather_sem.at[q])
+
+            @pl.when(midx // 4 != q)
+            def _():
+                wait_for(raw1.at[pl.ds(0, 16)], gather_sem.at[q])
 
             def scale(k, carry):
-                for lane in (2 * half, 2 * half + 1):
-                    block = raw1[lane * 16 + k].astype(F32) / den
+                for lane in range(4):
+                    block = raw1[k * 4 + lane].astype(F32) / den
                     y_own[0, pl.ds(k * 64, 64), lane * 128:(lane + 1) * 128] = block.astype(BF16)
                 return carry
 
-            lax.fori_loop(0, 16, scale, 0)
-            push(0, half).start()
-
-        def step(k, carry):
-            now = k % 2
+            lax.fori_loop(4 * q, 4 * q + 4, scale, 0)
+            push(0, q).start()
+
+        def scatter(slot, q):
+            def body(i, carry):
+                mm = 4 * q + (midx + i) % 4
+                for lane in range(4):
+                    @pl.when(jnp.logical_not(jnp.logical_and(mm == midx, lane == xpos)))
+                    def _():
+                        pltpu.make_async_remote_copy(
+                            y_own.at[slot, pl.ds(mm * 64, 64), pl.ds(lane * 128, 128)], res1.at[midx],
+                            out_send, result_sem.at[0],
+                            device_id=to(mm, 2 * lane + core), device_id_type=MESH).start()
+                return carry
+            lax.fori_loop(0, 4, body, 0)
+
+        def step(now, last):
             nxt = 1 - now
             a_own[now] = dot(y_own[now], y_own[now], TN).astype(BF16)
             push_gram(now).start()
-            for half in range(2):
-                push(now, half).wait()
-            a_cross[...] = dot(y_oth[now], y_own[now], TN).astype(BF16)
-            own_sq = dot(a_own[now], a_own[now], NN) + dot(a_cross[...], a_cross[...], TN)
-            b_own[...] = (NS_COEF_B * a_own[now].astype(F32) + NS_COEF_C * own_sq).astype(BF16)
+            square[...] = dot(a_own[now], a_own[now], NN)
+            cross = 0
+            for q in range(4):
+                push(now, q).wait()
+                rows = slice(q * 256, (q + 1) * 256)
+                cross = cross + dot(y_oth[now, rows], y_own[now, rows], TN)
+            a_cross[...] = cross.astype(BF16)
+            total = square[...] + dot(a_cross[...], a_cross[...], TN)
+            b_own[...] = (NS_COEF_B * a_own[now].astype(F32) + NS_COEF_C * total).astype(BF16)
+            square[...] = dot(a_cross[...], a_own[now], NN)
             push_gram(now).wait()
-            cross_sq = dot(a_cross[...], a_own[now], NN) + dot(a_oth[now], a_cross[...], NN)
-            b_cross[...] = (NS_COEF_B * a_cross[...].astype(F32) + NS_COEF_C * cross_sq).astype(BF16)
-            for half in range(2):
-                lanes = slice(half * 256, (half + 1) * 256)
-                update = dot(y_own[now], b_own[:, lanes], NN) + dot(y_oth[now], b_cross[:, lanes], NN)
-                y_own[nxt, :, lanes] = (NS_COEF_A * y_own[now, :, lanes].astype(F32) + update).astype(BF16)
-
-                @pl.when(k < NS_STEPS - 1)
-                def _():
-                    push(nxt, half).start()
-
-                @pl.when(k == NS_STEPS - 1)
-                def _():
-                    def scatter(i, carry):
-                        mm = (midx + i) % 16
-                        for lane in (2 * half, 2 * half + 1):
-                            @pl.when(jnp.logical_not(jnp.logical_and(mm == midx, lane == xpos)))
-                            def _():
-                                pltpu.make_async_remote_copy(
-                                    y_own.at[nxt, pl.ds(mm * 64, 64), pl.ds(lane * 128, 128)], res1.at[midx],
-                                    out_send, result_sem.at[0],
-                                    device_id=to(mm, 2 * lane + core), device_id_type=MESH).start()
-                        return carry
-                    lax.fori_loop(0, 16, scatter, 0)
+            total = square[...] + dot(a_oth[now], a_cross[...], NN)
+            b_cross[...] = (NS_COEF_B * a_cross[...].astype(F32) + NS_COEF_C * total).astype(BF16)
+            for q in range(4):
+                rows = slice(q * 256, (q + 1) * 256)
+                update = dot(y_own[now, rows], b_own[...], NN) + dot(y_oth[now, rows], b_cross[...], NN)
+                y_own[nxt, rows] = (NS_COEF_A * y_own[now, rows].astype(F32) + update).astype(BF16)
+                if last:
+                    scatter(nxt, q)
+                else:
+                    push(nxt, q).start()
+
+        def two_steps(k, carry):
+            step(0, False)
+            step(1, False)
             return carry
 
-        lax.fori_loop(0, NS_STEPS, step, 0)
+        lax.fori_loop(0, NS_STEPS // 2, two_steps, 0)
+        step(0, True)
         for lane in range(4):
             @pl.when(xpos == lane)
             def _():
@@ -273,11 +293,11 @@
             vmem((64, 64, 128), BF16), vmem((128, 32, 128), BF16), vmem((128, 1, 128), F32),
             vmem((2, 1024, 512), BF16), vmem((2, 1024, 512), BF16),
             vmem((2, 512, 512), BF16), vmem((512, 512), BF16), vmem((2, 512, 512), BF16),
-            vmem((512, 512), BF16), vmem((512, 512), BF16),
+            vmem((512, 512), BF16), vmem((512, 512), BF16), vmem((512, 512), F32),
             vmem((512, 1024), BF16), vmem((512, 512), BF16), vmem((512, 512), BF16),
-            sem((4,)), sem((4,)), sem((2,)), sem, sem((2,)), sem((2, 2)), sem((2, 2)), sem((2,)), sem((2,)), sem,
+            sem((4,)), sem((4,)), sem((4,)), sem, sem((2,)), sem((2, 4)), sem((2, 4)), sem((2,)), sem((2,)), sem,
         ],
-        compiler_params=pltpu.CompilerParams(collective_id=0, has_side_effects=True, vmem_limit_bytes=48 << 20),
+        compiler_params=pltpu.CompilerParams(collective_id=0, has_side_effects=True, vmem_limit_bytes=67043328),
         name='muon_exchange',
     )(m1, g1, m2, g2)
 

time: 73.6 us -> 61.9 us (0.84)
  the two profiles are of different devices: /device:TPU:6 before, /device:TPU:96 now
where the time goes in v2:
time: 61.9 us; the launch traced here: 61.8 us
  Pallas kernels  57.6 us (93%)
  other arithmetic  3.48 us (6%)
  between operations  0.69 us (1%)
    pallas_call x1, Pallas kernels, exchange(): pl.pallas_call(muon_kernel, out_shape=(jax.ShapeDtypeStruct((16, 64, 128)...  57.6 us
    sub x2, other arithmetic, weight_step(): return (weights - LEARN_RATE * (ortho + DECAY * weights), new_mom)  3.48 us

profile of v2, /device:TPU:96, one launch (start us, length us, event | category | flops | bytes accessed | tf_op | source)
XLA Modules:
  0.0 61.8 jit_solution(17118437801748237727)
XLA Ops:
  0.6 57.6 %muon_exchange.1 = (bf16[16,64,128]{2,1,0:T(8,128)(2,1)}, bf16[16,32,128]{2,1,0:T(8,128)(2,1)}) custom-call(f32[16,64,128]{2,1,0:T(8,128)} %bitcast.16, bf16[16,64,128]{2,1,0:T(8,128)(2,1)} %bitcast.17, f32[16,32,128]{2,1,0:T(8,128)} %bitcast.18, bf16[16,32,128]{2,1,0:T(8,128)(2,1)} %bitcast.19), custom_call_target="tpu_custom_call" | custom-call | tf_op jit(solution)/shard_map/muon_exchange/pallas_call | solution.py:285
  58.2 0.0 copy-start
  58.2 0.0 copy-start.1
  58.2 0.0 copy-start.2
  58.2 0.0 copy-start.3
  58.3 2.6 %fusion.1 = (f32[16,128,64]{1,2,0:T(8,128)}, f32[16,128,64]{1,2,0:T(8,128)}) fusion(f32[16,128,64]{1,2,0:T(8,128)} %param.6, bf16[16,64,128]{2,1,0:T(8,128)(2,1)} %get-tuple-element.6, bf16[16,128,64]{1,2,0:T(8,128)(2,1)} %param.8, f32[16,128,64]{1,2,0:T(8,128)} %param.7), kind=kLoop, calls=%fused_computation.2 | loop fusion | flops 1179648 | bytes 2621440 | tf_op jit(solution)/shard_map/sub | solution.py:308
  60.9 0.0 copy-done
  60.9 0.0 copy-done.1
  60.9 0.0 copy-done.2
  60.9 0.0 copy-done.3
  60.9 0.9 %fusion.3 = (f32[16,128,32]{1,2,0:T(8,128)}, f32[16,128,32]{1,2,0:T(8,128)}) fusion(f32[16,128,32]{1,2,0:T(8,128)S(1)} %copy-done.2, bf16[16,32,128]{2,1,0:T(8,128)(2,1)S(1)} %copy-done.3, bf16[16,128,32]{1,2,0:T(8,128)(2,1)S(1)} %copy-done.1, f32[16,128,32]{1,2,0:T(8,128)S(1)} %copy-done), kind=kLoop, calls=%fused_computation.6 | loop fusion | flops 589824 | bytes 1310720 | tf_op jit(solution)/shard_map/sub | solution.py:308
Async XLA Ops:
  58.2 2.7 %copy-start = (f32[16,128,32]{1,2,0:T(8,128)S(1)}, f32[16,128,32]{1,2,0:T(8,128)}, u32[]{:S(2)}) copy-start(f32[16,128,32]{1,2,0:T(8,128)} %param.10) | copy-start | bytes 786436
  58.2 2.6 %copy-start.1 = (bf16[16,128,32]{1,2,0:T(8,128)(2,1)S(1)}, bf16[16,128,32]{1,2,0:T(8,128)(2,1)}, u32[]{:S(2)}) copy-start(bf16[16,128,32]{1,2,0:T(8,128)(2,1)} %param.11) | copy-start | bytes 393220
  58.2 2.6 %copy-start.2 = (f32[16,128,32]{1,2,0:T(8,128)S(1)}, f32[16,128,32]{1,2,0:T(8,128)}, u32[]{:S(2)}) copy-start(f32[16,128,32]{1,2,0:T(8,128)} %param.9) | copy-start | bytes 786436
  58.2 2.6 %copy-start.3 = (bf16[16,32,128]{2,1,0:T(8,128)(2,1)S(1)}, bf16[16,32,128]{2,1,0:T(8,128)(2,1)}, u32[]{:S(2)}) copy-start(bf16[16,32,128]{2,1,0:T(8,128)(2,1)} %get-tuple-element.7) | copy-start | bytes 393220

commit v3 on v2

--- a/solution.py
+++ b/solution.py
@@ -22,15 +22,16 @@
 TN = ((0,), (0,))
 NT = ((1,), (1,))
 MESH = pl.DeviceIdType.MESH
+SCALE = 0.2 * math.sqrt(1024)
 
 
 def dot(lhs, rhs, dims):
     return lax.dot_general(lhs, rhs, (dims, ((), ())), preferred_element_type=F32)
 
 
-def muon_kernel(m1_hbm, g1_hbm, m2_hbm, g2_hbm, res1, res2,
-                m1, g1, m2, g2, send1, send2, part1, part2,
-                raw1, raw2, norms, y_own, y_oth, a_own, a_cross, a_oth, b_own, b_cross, square, y2, a2, b2,
+def muon_kernel(m1_hbm, g1_hbm, m2_hbm, g2_hbm, w1_hbm, w2_hbm, new_w1, new_m1, new_w2, new_m2,
+                m1, g1, m2, g2, w1, w2, res1, res2, send1, send2, part1, part2,
+                raw1, raw2, norms, half_norm, y_own, y_oth, a_own, a_cross, a_oth, b_own, b_cross, square, y2, a2, b2,
                 in_sem, send_sem, gather_sem, norm_sem, result_sem, y_send, y_recv, a_send, a_recv, out_send):
     midx = lax.axis_index('model')
     didx = lax.axis_index('data')
@@ -45,8 +46,9 @@
         return {'model': model, 'data': data}
 
     loads = [pltpu.make_async_copy(src, dst, in_sem.at[i])
-             for i, (src, dst) in enumerate(((m1_hbm, m1), (g1_hbm, g1), (m2_hbm, m2), (g2_hbm, g2)))]
-    for load in loads:
+             for i, (src, dst) in enumerate((
+                 (m1_hbm, m1), (g1_hbm, g1), (m2_hbm, m2), (g2_hbm, g2), (w1_hbm, w1), (w2_hbm, w2)))]
+    for load in loads[:4]:
         load.start()
 
     barrier = pltpu.get_barrier_semaphore()
@@ -56,49 +58,67 @@
         pl.semaphore_signal(barrier, inc=1, device_id=to(other // 8, other % 8), device_id_type=MESH)
         return carry
 
-    is_owner = jnp.logical_or(is_own1, is_own2)
-
-    @pl.when(is_owner)
+    @pl.when(is_own1)
+    def _():
+        def greet_side(i, carry):
+            other = (flat + 2 * i) % 128
+            pl.semaphore_signal(barrier, inc=1, device_id=to(other // 8, other % 8), device_id_type=MESH)
+            return carry
+
+        lax.fori_loop(1, 64, greet_side, 0)
+        pl.semaphore_signal(barrier, inc=1, device_id=to(midx, 2 * xpos + 1 - core), device_id_type=MESH)
+
+    @pl.when(is_own2)
     def _():
         lax.fori_loop(1, 128, greet, 0)
 
-    def momentum(e, carry, m_ref, g_ref, send, part):
+    def momentum(e, carry, m_ref, g_ref, new_m, send, part):
         value = MOMENTUM * m_ref[e] + g_ref[e].astype(F32)
+        new_m[e] = value
         send[e] = value.astype(BF16)
         part[e] = jnp.sum(value * value, axis=0, keepdims=True)
         return carry
 
     loads[0].wait()
     loads[1].wait()
-    lax.fori_loop(0, 16, functools.partial(momentum, m_ref=m1, g_ref=g1, send=send1, part=part1), 0)
+    lax.fori_loop(0, 16, functools.partial(momentum, m_ref=m1, g_ref=g1, new_m=new_m1, send=send1, part=part1), 0)
     loads[2].wait()
     loads[3].wait()
-    lax.fori_loop(0, 16, functools.partial(momentum, m_ref=m2, g_ref=g2, send=send2, part=part2), 0)
-
-    @pl.when(is_owner)
-    def _():
-        pl.semaphore_wait(barrier, 47)
-
-    @pl.when(jnp.logical_not(is_owner))
-    def _():
-        pl.semaphore_wait(barrier, 48)
-
-    def send_fc1(i, carry):
+    lax.fori_loop(0, 16, functools.partial(momentum, m_ref=m2, g_ref=g2, new_m=new_m2, send=send2, part=part2), 0)
+
+    @pl.when(is_own2)
+    def _():
+        pl.semaphore_wait(barrier, 31)
+
+    @pl.when(jnp.logical_not(is_own2))
+    def _():
+        pl.semaphore_wait(barrier, 32)
+
+    def owner_fc1(i):
         e = (midx + 2 * didx + i) % 16
         ox = (8 - e // 4 - e % 4) % 4
-        mine = jnp.logical_and(e == midx, is_own1)
-        for side in range(2):
-            @pl.when(jnp.logical_not(jnp.logical_and(mine, core == side)))
-            def _():
-                pltpu.make_async_remote_copy(
-                    part1.at[e], norms.at[flat], send_sem.at[1], norm_sem,
-                    device_id=to(e, 2 * ox + side), device_id_type=MESH).start()
-
-        @pl.when(jnp.logical_not(mine))
+        return e, jnp.logical_not(jnp.logical_and(e == midx, is_own1)), to(e, 2 * ox + core)
+
+    def send_norm1(i, carry):
+        e, away, owner = owner_fc1(i)
+
+        @pl.when(away)
+        def _():
+            pltpu.make_async_remote_copy(
+                part1.at[e], norms.at[midx * 4 + xpos], send_sem.at[1], norm_sem.at[0],
+                device_id=owner, device_id_type=MESH).start()
+        return carry
+
+    lax.fori_loop(0, 16, send_norm1, 0)
+
+    def send_fc1(i, carry):
+        e, away, owner = owner_fc1(i)
+
+        @pl.when(away)
         def _():
             pltpu.make_async_remote_copy(
                 send1.at[e], raw1.at[midx * 4 + xpos], send_sem.at[0], gather_sem.at[midx // 4],
-                device_id=to(e, 2 * ox + core), device_id_type=MESH).start()
+                device_id=owner, device_id_type=MESH).start()
         return carry
 
     lax.fori_loop(0, 16, send_fc1, 0)
@@ -110,7 +130,7 @@
         @pl.when(jnp.logical_not(jnp.logical_and(e == midx, is_own2)))
         def _():
             pltpu.make_async_remote_copy(
-                part2.at[e], norms.at[flat], send_sem.at[3], norm_sem,
+                part2.at[e], norms.at[flat], send_sem.at[3], norm_sem.at[0],
                 device_id=to(e, 2 * ox + 1), device_id_type=MESH).start()
             pltpu.make_async_remote_copy(
                 send2.at[e], raw2.at[flat], send_sem.at[2], gather_sem.at[0],
@@ -118,21 +138,27 @@
         return carry
 
     lax.fori_loop(0, 16, send_fc2, 0)
+    for load in loads[4:]:
+        load.start()
 
     def wait_for(ref, sem):
         pltpu.make_async_copy(ref, ref, sem).wait()
 
-    def denominator():
-        wait_for(norms.at[pl.ds(0, 127)], norm_sem)
-        total = jnp.sum(jnp.sum(norms[...], axis=0), axis=1, keepdims=True)
-        return jnp.sqrt(total) + NORM_EPS
+    def inverse_norm(total):
+        return 1.0 / (jnp.sqrt(jnp.sum(total, axis=1, keepdims=True)) + NORM_EPS)
 
     @pl.when(is_own1)
     def _():
         partner = to(midx, 2 * xpos + 1 - core)
-        norms[flat] = part1[midx]
+        norms[midx * 4 + xpos] = part1[midx]
         raw1[midx * 4 + xpos] = send1[midx]
-        den = denominator()
+        wait_for(norms.at[pl.ds(0, 63)], norm_sem.at[0])
+        half_norm[0] = jnp.sum(norms[:64], axis=0)
+        swap = pltpu.make_async_remote_copy(
+            half_norm.at[0], half_norm.at[1], norm_sem.at[1], norm_sem.at[2], device_id=partner, device_id_type=MESH)
+        swap.start()
+        swap.wait()
+        inv = inverse_norm(half_norm[0] + half_norm[1])
 
         def push(slot, q):
             rows = (slot, pl.ds(q * 256, 256))
@@ -156,7 +182,7 @@
 
             def scale(k, carry):
                 for lane in range(4):
-                    block = raw1[k * 4 + lane].astype(F32) / den
+                    block = raw1[k * 4 + lane].astype(F32) * inv
                     y_own[0, pl.ds(k * 64, 64), lane * 128:(lane + 1) * 128] = block.astype(BF16)
                 return carry
 
@@ -215,24 +241,24 @@
                 res1[midx] = y_own[NS_STEPS % 2, pl.ds(midx * 64, 64), lane * 128:(lane + 1) * 128]
         wait_for(raw1.at[pl.ds(0, 63)], out_send)
         wait_for(send1.at[pl.ds(0, 15)], send_sem.at[0])
-        wait_for(norms.at[pl.ds(0, 31)], send_sem.at[1])
-        wait_for(res1.at[pl.ds(0, 15)], result_sem.at[0])
+        wait_for(norms.at[pl.ds(0, 15)], send_sem.at[1])
 
     @pl.when(jnp.logical_not(is_own1))
     def _():
         wait_for(send1, send_sem.at[0])
-        wait_for(norms.at[pl.ds(0, 32)], send_sem.at[1])
+        wait_for(norms.at[pl.ds(0, 16)], send_sem.at[1])
 
     @pl.when(is_own2)
     def _():
         norms[flat] = part2[midx]
         raw2[flat] = send2[midx]
-        den = denominator()
+        wait_for(norms.at[pl.ds(0, 127)], norm_sem.at[0])
+        inv = inverse_norm(jnp.sum(norms[...], axis=0))
         wait_for(raw2.at[pl.ds(0, 127)], gather_sem.at[0])
 
         def scale(k, carry):
             for d in range(8):
-                block = raw2[k * 8 + d].astype(F32) / den
+                block = raw2[k * 8 + d].astype(F32) * inv
                 y2[pl.ds(k * 32, 32), d * 128:(d + 1) * 128] = block.astype(BF16)
             return carry
 
@@ -264,58 +290,81 @@
         wait_for(raw2.at[pl.ds(0, 127)], out_send)
         wait_for(send2.at[pl.ds(0, 15)], send_sem.at[2])
         wait_for(norms.at[pl.ds(0, 15)], send_sem.at[3])
-        wait_for(res2.at[pl.ds(0, 15)], result_sem.at[1])
 
     @pl.when(jnp.logical_not(is_own2))
     def _():
         wait_for(send2, send_sem.at[2])
         wait_for(norms.at[pl.ds(0, 16)], send_sem.at[3])
-        wait_for(res2, result_sem.at[1])
-
-    @pl.when(jnp.logical_not(is_own1))
-    def _():
-        wait_for(res1, result_sem.at[0])
-
-
-def exchange(m1, g1, m2, g2):
+
+    def weight_step(e, carry, w_ref, res, new_w, scale):
+        old = w_ref[e]
+        new_w[e] = old - LEARN_RATE * (res[e].astype(F32) * scale + DECAY * old)
+        return carry
+
+    for index, mine, res, w_ref, new_w, scale in (
+            (1, is_own2, res2, w2, new_w2, SCALE), (0, is_own1, res1, w1, new_w1, SCALE)):
+        @pl.when(mine)
+        def _():
+            wait_for(res.at[pl.ds(0, 15)], result_sem.at[index])
+
+        @pl.when(jnp.logical_not(mine))
+        def _():
+            wait_for(res, result_sem.at[index])
+
+        loads[5 if index else 4].wait()
+        lax.fori_loop(0, 16, functools.partial(weight_step, w_ref=w_ref, res=res, new_w=new_w, scale=scale), 0)
+
+
+def store_kernel(*refs):
+    sem = refs[8]
+    copies = [pltpu.make_async_copy(refs[i], refs[4 + i], sem.at[i]) for i in range(4)]
+    for copy in copies:
+        copy.start()
+    for copy in copies:
+        copy.wait()
+
+
+def local_update(w1, m1, g1, w2, m2, g2):
     hbm_spec = pl.BlockSpec(memory_space=pltpu.HBM)
     vmem_spec = pl.BlockSpec(memory_space=pltpu.VMEM)
     vmem = pltpu.VMEM
     sem = pltpu.SemaphoreType.DMA
-    return pl.pallas_call(
+    big, small = (16, 64, 128), (16, 32, 128)
+    outs = tuple(jax.ShapeDtypeStruct(shape, F32) for shape in (big, big, small, small))
+    operands = (pltpu.with_memory_space_constraint(x, pltpu.HBM) for x in (m1, g1, m2, g2, w1, w2))
+    updated = pl.pallas_call(
         muon_kernel,
-        out_shape=(jax.ShapeDtypeStruct((16, 64, 128), BF16), jax.ShapeDtypeStruct((16, 32, 128), BF16)),
-        in_specs=[hbm_spec] * 4,
-        out_specs=(vmem_spec, vmem_spec),
+        out_shape=outs,
+        in_specs=[hbm_spec] * 6,
+        out_specs=(vmem_spec,) * 4,
         scratch_shapes=[
-            vmem((16, 64, 128), F32), vmem((16, 64, 128), BF16), vmem((16, 32, 128), F32), vmem((16, 32, 128), BF16),
-            vmem((16, 64, 128), BF16), vmem((16, 32, 128), BF16), vmem((16, 1, 128), F32), vmem((16, 1, 128), F32),
-            vmem((64, 64, 128), BF16), vmem((128, 32, 128), BF16), vmem((128, 1, 128), F32),
+            vmem(big, F32), vmem(big, BF16), vmem(small, F32), vmem(small, BF16), vmem(big, F32), vmem(small, F32),
+            vmem(big, BF16), vmem(small, BF16),
+            vmem(big, BF16), vmem(small, BF16), vmem((16, 1, 128), F32), vmem((16, 1, 128), F32),
+            vmem((64, 64, 128), BF16), vmem((128, 32, 128), BF16), vmem((128, 1, 128), F32), vmem((2, 1, 128), F32),
             vmem((2, 1024, 512), BF16), vmem((2, 1024, 512), BF16),
             vmem((2, 512, 512), BF16), vmem((512, 512), BF16), vmem((2, 512, 512), BF16),
             vmem((512, 512), BF16), vmem((512, 512), BF16), vmem((512, 512), F32),
             vmem((512, 1024), BF16), vmem((512, 512), BF16), vmem((512, 512), BF16),
-            sem((4,)), sem((4,)), sem((4,)), sem, sem((2,)), sem((2, 4)), sem((2, 4)), sem((2,)), sem((2,)), sem,
+            sem((6,)), sem((4,)), sem((4,)), sem((3,)), sem((2,)), sem((2, 4)), sem((2, 4)), sem((2,)), sem((2,)), sem,
         ],
-        compiler_params=pltpu.CompilerParams(collective_id=0, has_side_effects=True, vmem_limit_bytes=67043328),
+        compiler_params=pltpu.CompilerParams(collective_id=0, has_side_effects=True, vmem_limit_bytes=40 << 20),
         name='muon_exchange',
-    )(m1, g1, m2, g2)
-
-
-def weight_step(weights, momentum, gradient, ortho_t, rows, cols):
-    new_mom = MOMENTUM * momentum + gradient.astype(F32)
-    ortho = jnp.swapaxes(ortho_t, 1, 2).astype(F32) * (0.2 * math.sqrt(max(rows, cols)))
-    return weights - LEARN_RATE * (ortho + DECAY * weights), new_mom
+    )(*operands)
+    return pl.pallas_call(
+        store_kernel,
+        out_shape=outs,
+        in_specs=[vmem_spec] * 4,
+        out_specs=(hbm_spec,) * 4,
+        scratch_shapes=[sem((4,))],
+        name='store_outputs',
+    )(*(pltpu.with_memory_space_constraint(x, pltpu.VMEM) for x in updated))
 
 
 def solution(mesh):
     block_spec = P('stage', 'data', 'model')
 
-    def local_step(w1, m1, g1, w2, m2, g2):
-        flip = functools.partial(jnp.swapaxes, axis1=1, axis2=2)
-        ortho1, ortho2 = exchange(flip(m1), flip(g1), flip(m2), flip(g2))
-        new_w1, new_m1 = weight_step(w1, m1, g1, ortho1, 1024, 1024)
-        new_w2, new_m2 = weight_step(w2, m2, g2, ortho2, 1024, 512)
-        return new_w1, new_m1, new_w2, new_m2
+    def local_step(*args):
+        return tuple(jnp.swapaxes(out, 1, 2) for out in local_update(*(jnp.swapaxes(arg, 1, 2) for arg in args)))
 
     return jax.shard_map(local_step, mesh=mesh, in_specs=(block_spec,) * 6, out_specs=(block_spec,) * 4, check_vma=False)

time: 61.9 us -> 57.6 us (0.931)
  other arithmetic: 3.48 us -> 0 us
  Pallas kernels: 57.6 us -> 56.8 us
    sub x2 -> x0, other arithmetic: 3.48 us -> none  [weight_step(): return (weights - LEARN_RATE * (ortho + DECAY * weights), new_mom)]
    pallas_call x1 -> x2, Pallas kernels: 57.6 us -> 56.8 us  [the longest x1 55.7 us: local_update(): pl.pallas_call(muon_kernel, out_shape=outs, in_specs=[hbm_spec] * 6, out_...]
where the time goes in v3:
time: 57.6 us; the launch traced here: 57.5 us
  Pallas kernels  56.8 us (99%)
  between operations  0.64 us (1%)
    pallas_call x1, Pallas kernels, local_update(): pl.pallas_call(muon_kernel, out_shape=outs, in_specs=[hbm_spec] * 6, out_...  55.7 us
    pallas_call x1, Pallas kernels, local_update(): pl.pallas_call(store_kernel, out_shape=outs, in_specs=[vmem_spec] * 4, ou...  1.17 us

profile of v3, /device:TPU:96, one launch (start us, length us, event | category | flops | bytes accessed | tf_op | source)
XLA Modules:
  0.0 57.5 jit_solution(6123811217096799108)
XLA Ops:
  0.6 55.7 %muon_exchange.1 = (f32[16,64,128]{2,1,0:T(8,128)S(1)}, f32[16,64,128]{2,1,0:T(8,128)S(1)}, f32[16,32,128]{2,1,0:T(8,128)S(1)}, f32[16,32,128]{2,1,0:T(8,128)S(1)}) custom-call(f32[16,64,128]{2,1,0:T(8,128)} %bitcast.10, bf16[16,64,128]{2,1,0:T(8,128)(2,1)} %bitcast.12, f32[16,32,128]{2,1,0:T(8,128)} %bitcast.13, bf16[16,32,128]{2,1,0:T(8,128)(2,1)} %bitcast.15, ...), custom_call_target="tpu_custom_call" | custom-call | tf_op jit(solution)/shard_map/muon_exchange/pallas_call | solution.py:335
  56.3 1.2 %store_outputs.1 = (f32[16,64,128]{2,1,0:T(8,128)}, f32[16,64,128]{2,1,0:T(8,128)}, f32[16,32,128]{2,1,0:T(8,128)}, f32[16,32,128]{2,1,0:T(8,128)}) custom-call(f32[16,64,128]{2,1,0:T(8,128)S(1)} %get-tuple-element.12.refs_0_, f32[16,64,128]{2,1,0:T(8,128)S(1)} %get-tuple-element.13.refs_1_, f32[16,32,128]{2,1,0:T(8,128)S(1)} %get-tuple-element.14.refs_2_, ...), custom_call_target="tpu_custom_call" | custom-call | tf_op jit(solution)/shard_map/store_outputs/pallas_call | solution.py:354

commit v4 on v3

--- a/solution.py
+++ b/solution.py
@@ -31,8 +31,8 @@
 
 def muon_kernel(m1_hbm, g1_hbm, m2_hbm, g2_hbm, w1_hbm, w2_hbm, new_w1, new_m1, new_w2, new_m2,
                 m1, g1, m2, g2, w1, w2, res1, res2, send1, send2, part1, part2,
-                raw1, raw2, norms, half_norm, y_own, y_oth, a_own, a_cross, a_oth, b_own, b_cross, square, y2, a2, b2,
-                in_sem, send_sem, gather_sem, norm_sem, result_sem, y_send, y_recv, a_send, a_recv, out_send):
+                raw1, raw2, norms, half_norm, relay, y_own, y_oth, a_own, a_cross, a_oth, b_own, b_cross, square, y2, a2, b2,
+                in_sem, send_sem, gather_sem, norm_sem, relay_sem, result_sem, y_send, y_recv, a_send, a_recv, out_send):
     midx = lax.axis_index('model')
     didx = lax.axis_index('data')
     core = didx % 2
@@ -81,10 +81,7 @@
 
     loads[0].wait()
     loads[1].wait()
-    lax.fori_loop(0, 16, functools.partial(momentum, m_ref=m1, g_ref=g1, new_m=new_m1, send=send1, part=part1), 0)
-    loads[2].wait()
-    loads[3].wait()
-    lax.fori_loop(0, 16, functools.partial(momentum, m_ref=m2, g_ref=g2, new_m=new_m2, send=send2, part=part2), 0)
+    lax.fori_loop(0, 16, functools.partial(momentum, m_ref=m1, g_ref=g1, new_m=new_m1, send=send1, part=part1), 0, unroll=True)
 
     @pl.when(is_own2)
     def _():
@@ -109,7 +106,7 @@
                 device_id=owner, device_id_type=MESH).start()
         return carry
 
-    lax.fori_loop(0, 16, send_norm1, 0)
+    lax.fori_loop(0, 16, send_norm1, 0, unroll=True)
 
     def send_fc1(i, carry):
         e, away, owner = owner_fc1(i)
@@ -121,7 +118,11 @@
                 device_id=owner, device_id_type=MESH).start()
         return carry
 
-    lax.fori_loop(0, 16, send_fc1, 0)
+    lax.fori_loop(0, 16, send_fc1, 0, unroll=True)
+
+    loads[2].wait()
+    loads[3].wait()
+    lax.fori_loop(0, 16, functools.partial(momentum, m_ref=m2, g_ref=g2, new_m=new_m2, send=send2, part=part2), 0)
 
     def send_fc2(i, carry):
         e = (midx + 2 * didx + i) % 16
@@ -186,21 +187,37 @@
                     y_own[0, pl.ds(k * 64, 64), lane * 128:(lane + 1) * 128] = block.astype(BF16)
                 return carry
 
-            lax.fori_loop(4 * q, 4 * q + 4, scale, 0)
+            lax.fori_loop(4 * q, 4 * q + 4, scale, 0, unroll=True)
             push(0, q).start()
 
         def scatter(slot, q):
             def body(i, carry):
                 mm = 4 * q + (midx + i) % 4
-                for lane in range(4):
-                    @pl.when(jnp.logical_not(jnp.logical_and(mm == midx, lane == xpos)))
-                    def _():
+                rows = (slot, pl.ds(mm * 64, 64))
+                far = pl.multiple_of((xpos + 2) % 4 * 128, 128)
+
+                @pl.when(mm != midx)
+                def _():
+                    pltpu.make_async_remote_copy(
+                        y_own.at[(*rows, pl.ds(far, 128))], relay.at[midx // 4], out_send, relay_sem.at[midx // 4],
+                        device_id=to(mm, 2 * xpos + core), device_id_type=MESH).start()
+
+                for hop in (1, 3, 0, 2):
+                    lane = (xpos + hop) % 4
+                    direct = {0: mm != midx, 2: mm == midx}.get(hop)
+
+                    def send():
                         pltpu.make_async_remote_copy(
-                            y_own.at[slot, pl.ds(mm * 64, 64), pl.ds(lane * 128, 128)], res1.at[midx],
+                            y_own.at[(*rows, pl.ds(pl.multiple_of(lane * 128, 128), 128))], res1.at[midx],
                             out_send, result_sem.at[0],
                             device_id=to(mm, 2 * lane + core), device_id_type=MESH).start()
+
+                    if direct is None:
+                        send()
+                    else:
+                        pl.when(direct)(send)
                 return carry
-            lax.fori_loop(0, 4, body, 0)
+            lax.fori_loop(0, 4, body, 0, unroll=True)
 
         def step(now, last):
             nxt = 1 - now
@@ -301,8 +318,7 @@
         new_w[e] = old - LEARN_RATE * (res[e].astype(F32) * scale + DECAY * old)
         return carry
 
-    for index, mine, res, w_ref, new_w, scale in (
-            (1, is_own2, res2, w2, new_w2, SCALE), (0, is_own1, res1, w1, new_w1, SCALE)):
+    def finish(index, mine, res, w_ref, new_w):
         @pl.when(mine)
         def _():
             wait_for(res.at[pl.ds(0, 15)], result_sem.at[index])
@@ -311,8 +327,32 @@
         def _():
             wait_for(res, result_sem.at[index])
 
-        loads[5 if index else 4].wait()
-        lax.fori_loop(0, 16, functools.partial(weight_step, w_ref=w_ref, res=res, new_w=new_w, scale=scale), 0)
+        loads[4 + index].wait()
+        lax.fori_loop(0, 16, functools.partial(weight_step, w_ref=w_ref, res=res, new_w=new_w, scale=SCALE), 0, unroll=True)
+
+    finish(1, is_own2, res2, w2, new_w2)
+
+    def forward(j, carry):
+        e = 4 * j + (8 - xpos - j) % 4
+
+        @pl.when(e != midx)
+        def _():
+            wait_for(relay.at[j], relay_sem.at[j])
+            pltpu.make_async_remote_copy(
+                relay.at[j], res1.at[e], relay_sem.at[4], result_sem.at[0],
+                device_id=to(midx, 2 * ((xpos + 2) % 4) + core), device_id_type=MESH).start()
+        return carry
+
+    lax.fori_loop(0, 4, forward, 0)
+    finish(0, is_own1, res1, w1, new_w1)
+
+    @pl.when(is_own1)
+    def _():
+        wait_for(relay.at[pl.ds(0, 3)], relay_sem.at[4])
+
+    @pl.when(jnp.logical_not(is_own1))
+    def _():
+        wait_for(relay, relay_sem.at[4])
 
 
 def store_kernel(*refs):
@@ -341,12 +381,12 @@
             vmem(big, F32), vmem(big, BF16), vmem(small, F32), vmem(small, BF16), vmem(big, F32), vmem(small, F32),
             vmem(big, BF16), vmem(small, BF16),
             vmem(big, BF16), vmem(small, BF16), vmem((16, 1, 128), F32), vmem((16, 1, 128), F32),
-            vmem((64, 64, 128), BF16), vmem((128, 32, 128), BF16), vmem((128, 1, 128), F32), vmem((2, 1, 128), F32),
+            vmem((64, 64, 128), BF16), vmem((128, 32, 128), BF16), vmem((128, 1, 128), F32), vmem((2, 1, 128), F32), vmem((4, 64, 128), BF16),
             vmem((2, 1024, 512), BF16), vmem((2, 1024, 512), BF16),
             vmem((2, 512, 512), BF16), vmem((512, 512), BF16), vmem((2, 512, 512), BF16),
             vmem((512, 512), BF16), vmem((512, 512), BF16), vmem((512, 512), F32),
             vmem((512, 1024), BF16), vmem((512, 512), BF16), vmem((512, 512), BF16),
-            sem((6,)), sem((4,)), sem((4,)), sem((3,)), sem((2,)), sem((2, 4)), sem((2, 4)), sem((2,)), sem((2,)), sem,
+            sem((6,)), sem((4,)), sem((4,)), sem((3,)), sem((5,)), sem((2,)), sem((2, 4)), sem((2, 4)), sem((2,)), sem((2,)), sem,
         ],
         compiler_params=pltpu.CompilerParams(collective_id=0, has_side_effects=True, vmem_limit_bytes=40 << 20),
         name='muon_exchange',

time: 57.6 us -> 54.6 us (0.948)
  Pallas kernels: 56.8 us -> 53.6 us
    pallas_call x1, Pallas kernels: 55.7 us -> 52.4 us  [local_update(): pl.pallas_call(muon_kernel, out_shape=outs, in_specs=[hbm_spec] * 6, out_...]
where the time goes in v4:
time: 54.6 us; the launch traced here: 54.2 us
  Pallas kernels  53.6 us (98%)
  between operations  0.64 us (1%)
    pallas_call x1, Pallas kernels, local_update(): pl.pallas_call(muon_kernel, out_shape=outs, in_specs=[hbm_spec] * 6, out_...  52.4 us
    pallas_call x1, Pallas kernels, local_update(): pl.pallas_call(store_kernel, out_shape=outs, in_specs=[vmem_spec] * 4, ou...  1.17 us

profile of v4, /device:TPU:96, one launch (start us, length us, event | category | flops | bytes accessed | tf_op | source)
XLA Modules:
  0.0 54.2 jit_solution(18091475092689380052)
XLA Ops:
  0.6 52.4 %muon_exchange.1 = (f32[16,64,128]{2,1,0:T(8,128)S(1)}, f32[16,64,128]{2,1,0:T(8,128)S(1)}, f32[16,32,128]{2,1,0:T(8,128)S(1)}, f32[16,32,128]{2,1,0:T(8,128)S(1)}) custom-call(f32[16,64,128]{2,1,0:T(8,128)} %bitcast.10, bf16[16,64,128]{2,1,0:T(8,128)(2,1)} %bitcast.12, f32[16,32,128]{2,1,0:T(8,128)} %bitcast.13, bf16[16,32,128]{2,1,0:T(8,128)(2,1)} %bitcast.15, ...), custom_call_target="tpu_custom_call" | custom-call | tf_op jit(solution)/shard_map/muon_exchange/pallas_call | solution.py:375
  53.0 1.2 %store_outputs.1 = (f32[16,64,128]{2,1,0:T(8,128)}, f32[16,64,128]{2,1,0:T(8,128)}, f32[16,32,128]{2,1,0:T(8,128)}, f32[16,32,128]{2,1,0:T(8,128)}) custom-call(f32[16,64,128]{2,1,0:T(8,128)S(1)} %get-tuple-element.12.refs_0_, f32[16,64,128]{2,1,0:T(8,128)S(1)} %get-tuple-element.13.refs_1_, f32[16,32,128]{2,1,0:T(8,128)S(1)} %get-tuple-element.14.refs_2_, ...), custom_call_target="tpu_custom_call" | custom-call | tf_op jit(solution)/shard_map/store_outputs/pallas_call | solution.py:394

commit v5 on v4

--- a/solution.py
+++ b/solution.py
@@ -51,6 +51,9 @@
     for load in loads[:4]:
         load.start()
 
+    def wait_for(ref, sem):
+        pltpu.make_async_copy(ref, ref, sem).wait()
+
     barrier = pltpu.get_barrier_semaphore()
 
     def greet(i, carry):
@@ -65,12 +68,12 @@
             pl.semaphore_signal(barrier, inc=1, device_id=to(other // 8, other % 8), device_id_type=MESH)
             return carry
 
-        lax.fori_loop(1, 64, greet_side, 0)
+        lax.fori_loop(1, 64, greet_side, 0, unroll=True)
         pl.semaphore_signal(barrier, inc=1, device_id=to(midx, 2 * xpos + 1 - core), device_id_type=MESH)
 
     @pl.when(is_own2)
     def _():
-        lax.fori_loop(1, 128, greet, 0)
+        lax.fori_loop(1, 128, greet, 0, unroll=True)
 
     def momentum(e, carry, m_ref, g_ref, new_m, send, part):
         value = MOMENTUM * m_ref[e] + g_ref[e].astype(F32)
@@ -92,7 +95,8 @@
         pl.semaphore_wait(barrier, 32)
 
     def owner_fc1(i):
-        e = (midx + 2 * didx + i) % 16
+        hop = (2, 1, 3, 0)[i // 4]
+        e = 4 * ((midx // 4 + hop) % 4) + (midx + didx + i) % 4
         ox = (8 - e // 4 - e % 4) % 4
         return e, jnp.logical_not(jnp.logical_and(e == midx, is_own1)), to(e, 2 * ox + core)
 
@@ -106,7 +110,8 @@
                 device_id=owner, device_id_type=MESH).start()
         return carry
 
-    lax.fori_loop(0, 16, send_norm1, 0, unroll=True)
+    for i in range(16):
+        send_norm1(i, 0)
 
     def send_fc1(i, carry):
         e, away, owner = owner_fc1(i)
@@ -118,11 +123,20 @@
                 device_id=owner, device_id_type=MESH).start()
         return carry
 
-    lax.fori_loop(0, 16, send_fc1, 0, unroll=True)
+    for i in range(16):
+        send_fc1(i, 0)
 
     loads[2].wait()
     loads[3].wait()
     lax.fori_loop(0, 16, functools.partial(momentum, m_ref=m2, g_ref=g2, new_m=new_m2, send=send2, part=part2), 0)
+
+    @pl.when(is_own1)
+    def _():
+        wait_for(send1.at[pl.ds(0, 15)], send_sem.at[0])
+
+    @pl.when(jnp.logical_not(is_own1))
+    def _():
+        wait_for(send1, send_sem.at[0])
 
     def send_fc2(i, carry):
         e = (midx + 2 * didx + i) % 16
@@ -141,9 +155,6 @@
     lax.fori_loop(0, 16, send_fc2, 0)
     for load in loads[4:]:
         load.start()
-
-    def wait_for(ref, sem):
-        pltpu.make_async_copy(ref, ref, sem).wait()
 
     def inverse_norm(total):
         return 1.0 / (jnp.sqrt(jnp.sum(total, axis=1, keepdims=True)) + NORM_EPS)
@@ -162,7 +173,7 @@
         inv = inverse_norm(half_norm[0] + half_norm[1])
 
         def push(slot, q):
-            rows = (slot, pl.ds(q * 256, 256))
+            rows = (slot, pl.ds(pl.multiple_of(q * 256, 256), 256))
             return pltpu.make_async_remote_copy(
                 y_own.at[rows], y_oth.at[rows], y_send.at[slot, q], y_recv.at[slot, q],
                 device_id=partner, device_id_type=MESH)
@@ -172,23 +183,22 @@
                 a_own.at[slot], a_oth.at[slot], a_send.at[slot], a_recv.at[slot],
                 device_id=partner, device_id_type=MESH)
 
-        for q in range(4):
-            @pl.when(midx // 4 == q)
-            def _():
-                wait_for(raw1.at[pl.ds(0, 15)], gather_sem.at[q])
-
-            @pl.when(midx // 4 != q)
-            def _():
-                wait_for(raw1.at[pl.ds(0, 16)], gather_sem.at[q])
+        for hop in (0, 1, 3, 2):
+            q = (midx // 4 + hop) % 4
+            wait_for(raw1.at[pl.ds(0, 15 if hop == 0 else 16)], gather_sem.at[q])
 
             def scale(k, carry):
                 for lane in range(4):
                     block = raw1[k * 4 + lane].astype(F32) * inv
-                    y_own[0, pl.ds(k * 64, 64), lane * 128:(lane + 1) * 128] = block.astype(BF16)
+                    y_own[0, pl.ds(pl.multiple_of(k * 64, 64), 64), lane * 128:(lane + 1) * 128] = block.astype(BF16)
                 return carry
 
-            lax.fori_loop(4 * q, 4 * q + 4, scale, 0, unroll=True)
+            for k in range(4):
+                scale(4 * q + k, 0)
             push(0, q).start()
+            rows = pl.ds(pl.multiple_of(q * 256, 256), 256)
+            part = dot(y_own[0, rows], y_own[0, rows], TN)
+            square[...] = part if hop == 0 else square[...] + part
 
         def scatter(slot, q):
             def body(i, carry):
@@ -219,10 +229,12 @@
                 return carry
             lax.fori_loop(0, 4, body, 0, unroll=True)
 
+        def gram(slot, value):
+            a_own[slot] = value.astype(BF16)
+            push_gram(slot).start()
+
         def step(now, last):
             nxt = 1 - now
-            a_own[now] = dot(y_own[now], y_own[now], TN).astype(BF16)
-            push_gram(now).start()
             square[...] = dot(a_own[now], a_own[now], NN)
             cross = 0
             for q in range(4):
@@ -244,6 +256,10 @@
                     scatter(nxt, q)
                 else:
                     push(nxt, q).start()
+            if not last:
+                gram(nxt, dot(y_own[nxt], y_own[nxt], TN))
+
+        gram(0, square[...])
 
         def two_steps(k, carry):
             step(0, False)
@@ -256,13 +272,10 @@
             @pl.when(xpos == lane)
             def _():
                 res1[midx] = y_own[NS_STEPS % 2, pl.ds(midx * 64, 64), lane * 128:(lane + 1) * 128]
-        wait_for(raw1.at[pl.ds(0, 63)], out_send)
-        wait_for(send1.at[pl.ds(0, 15)], send_sem.at[0])
         wait_for(norms.at[pl.ds(0, 15)], send_sem.at[1])
 
     @pl.when(jnp.logical_not(is_own1))
     def _():
-        wait_for(send1, send_sem.at[0])
         wait_for(norms.at[pl.ds(0, 16)], send_sem.at[1])
 
     @pl.when(is_own2)
@@ -348,6 +361,7 @@
 
     @pl.when(is_own1)
     def _():
+        wait_for(raw1.at[pl.ds(0, 63)], out_send)
         wait_for(relay.at[pl.ds(0, 3)], relay_sem.at[4])
 
     @pl.when(jnp.logical_not(is_own1))

time: 54.6 us -> 53.2 us (0.974)
  Pallas kernels: 53.6 us -> 52.2 us
    pallas_call x1, Pallas kernels: 52.4 us -> 51 us  [local_update(): pl.pallas_call(muon_kernel, out_shape=outs, in_specs=[hbm_spec] * 6, out_...]
where the time goes in v5:
time: 53.2 us; the launch traced here: 53 us
  Pallas kernels  52.2 us (98%)
  between operations  0.82 us (2%)
    pallas_call x1, Pallas kernels, local_update(): pl.pallas_call(muon_kernel, out_shape=outs, in_specs=[hbm_spec] * 6, out_...  51 us
    pallas_call x1, Pallas kernels, local_update(): pl.pallas_call(store_kernel, out_shape=outs, in_specs=[vmem_spec] * 4, ou...  1.17 us

profile of v5, /device:TPU:96, one launch (start us, length us, event | category | flops | bytes accessed | tf_op | source)
XLA Modules:
  0.0 53.0 jit_solution(1029838327843360996)
XLA Ops:
  0.6 51.0 %muon_exchange.1 = (f32[16,64,128]{2,1,0:T(8,128)S(1)}, f32[16,64,128]{2,1,0:T(8,128)S(1)}, f32[16,32,128]{2,1,0:T(8,128)S(1)}, f32[16,32,128]{2,1,0:T(8,128)S(1)}) custom-call(f32[16,64,128]{2,1,0:T(8,128)} %bitcast.10, bf16[16,64,128]{2,1,0:T(8,128)(2,1)} %bitcast.12, f32[16,32,128]{2,1,0:T(8,128)} %bitcast.13, bf16[16,32,128]{2,1,0:T(8,128)(2,1)} %bitcast.15, ...), custom_call_target="tpu_custom_call" | custom-call | tf_op jit(solution)/shard_map/muon_exchange/pallas_call | solution.py:389
  51.7 1.2 %store_outputs.1 = (f32[16,64,128]{2,1,0:T(8,128)}, f32[16,64,128]{2,1,0:T(8,128)}, f32[16,32,128]{2,1,0:T(8,128)}, f32[16,32,128]{2,1,0:T(8,128)}) custom-call(f32[16,64,128]{2,1,0:T(8,128)S(1)} %get-tuple-element.12.refs_0_, f32[16,64,128]{2,1,0:T(8,128)S(1)} %get-tuple-element.13.refs_1_, f32[16,32,128]{2,1,0:T(8,128)S(1)} %get-tuple-element.14.refs_2_, ...), custom_call_target="tpu_custom_call" | custom-call | tf_op jit(solution)/shard_map/store_outputs/pallas_call | solution.py:408

commit v6 on v5

--- a/solution.py
+++ b/solution.py
@@ -201,9 +201,12 @@
             square[...] = part if hop == 0 else square[...] + part
 
         def scatter(slot, q):
-            def body(i, carry):
-                mm = 4 * q + (midx + i) % 4
-                rows = (slot, pl.ds(mm * 64, 64))
+            def place(i):
+                mm = 4 * q + i
+                return mm, (slot, pl.ds(mm * 64, 64))
+
+            for i in range(4):
+                mm, rows = place(i)
                 far = pl.multiple_of((xpos + 2) % 4 * 128, 128)
 
                 @pl.when(mm != midx)
@@ -212,6 +215,8 @@
                         y_own.at[(*rows, pl.ds(far, 128))], relay.at[midx // 4], out_send, relay_sem.at[midx // 4],
                         device_id=to(mm, 2 * xpos + core), device_id_type=MESH).start()
 
+            for i in range(4):
+                mm, rows = place(i)
                 for hop in (1, 3, 0, 2):
                     lane = (xpos + hop) % 4
                     direct = {0: mm != midx, 2: mm == midx}.get(hop)
@@ -226,8 +231,6 @@
                         send()
                     else:
                         pl.when(direct)(send)
-                return carry
-            lax.fori_loop(0, 4, body, 0, unroll=True)
 
         def gram(slot, value):
             a_own[slot] = value.astype(BF16)

time: 53.2 us -> 52.7 us (level)
  no operation moved by 1% of the time
where the time goes in v6:
time: 52.7 us; the launch traced here: 52.6 us
  Pallas kernels  51.8 us (98%)
  between operations  0.82 us (2%)
    pallas_call x1, Pallas kernels, local_update(): pl.pallas_call(muon_kernel, out_shape=outs, in_specs=[hbm_spec] * 6, out_...  50.6 us
    pallas_call x1, Pallas kernels, local_update(): pl.pallas_call(store_kernel, out_shape=outs, in_specs=[vmem_spec] * 4, ou...  1.17 us

profile of v6, /device:TPU:96, one launch (start us, length us, event | category | flops | bytes accessed | tf_op | source)
XLA Modules:
  0.0 52.6 jit_solution(16782494011764007127)
XLA Ops:
  0.6 50.6 %muon_exchange.1 = (f32[16,64,128]{2,1,0:T(8,128)S(1)}, f32[16,64,128]{2,1,0:T(8,128)S(1)}, f32[16,32,128]{2,1,0:T(8,128)S(1)}, f32[16,32,128]{2,1,0:T(8,128)S(1)}) custom-call(f32[16,64,128]{2,1,0:T(8,128)} %bitcast.10, bf16[16,64,128]{2,1,0:T(8,128)(2,1)} %bitcast.12, f32[16,32,128]{2,1,0:T(8,128)} %bitcast.13, bf16[16,32,128]{2,1,0:T(8,128)(2,1)} %bitcast.15, ...), custom_call_target="tpu_custom_call" | custom-call | tf_op jit(solution)/shard_map/muon_exchange/pallas_call | solution.py:392
  51.2 1.2 %store_outputs.1 = (f32[16,64,128]{2,1,0:T(8,128)}, f32[16,64,128]{2,1,0:T(8,128)}, f32[16,32,128]{2,1,0:T(8,128)}, f32[16,32,128]{2,1,0:T(8,128)}) custom-call(f32[16,64,128]{2,1,0:T(8,128)S(1)} %get-tuple-element.12.refs_0_, f32[16,64,128]{2,1,0:T(8,128)S(1)} %get-tuple-element.13.refs_1_, f32[16,32,128]{2,1,0:T(8,128)S(1)} %get-tuple-element.14.refs_2_, ...), custom_call_target="tpu_custom_call" | custom-call | tf_op jit(solution)/shard_map/store_outputs/pallas_call | solution.py:411
